TPU v7x, 32 devices: a whole 2x2x4 slice. The times are simulated.
32 devices in a mesh: rep: 4 (over x, y), dp: 8 (over z, core).
Axes of the slice: x: 2, y: 2, z: 4, core: 2. Of those that a mesh axis runs over, the one named last changes fastest.
Arguments:
- g_w_gate: bfloat16 [32, 2, 1024, 3328], P(('rep', 'dp')), parts along dimension 0
- g_w_up: bfloat16 [32, 2, 1024, 3328], P(('rep', 'dp')), parts along dimension 0
- g_w_down: bfloat16 [32, 2, 3328, 1024], P(('rep', 'dp')), parts along dimension 0
- w_gate: bfloat16 [2, 1024, 3328], replicated
- w_up: bfloat16 [2, 1024, 3328], replicated
- w_down: bfloat16 [2, 3328, 1024], replicated
- m_w_gate: float32 [2, 1024, 3328], P(None, 'dp')
- m_w_up: float32 [2, 1024, 3328], P(None, 'dp')
- m_w_down: float32 [2, 3328, 1024], P(None, 'dp')
- v_w_gate: float32 [2, 1024, 3328], P(None, 'dp')
- v_w_up: float32 [2, 1024, 3328], P(None, 'dp')
- v_w_down: float32 [2, 3328, 1024], P(None, 'dp')
Outputs:
- output 1: bfloat16 [8, 1024, 3328], P('rep'), parts along dimension 0
- output 2: bfloat16 [8, 1024, 3328], P('rep'), parts along dimension 0
- output 3: bfloat16 [8, 3328, 1024], P('rep'), parts along dimension 0
- output 4: float32 [8, 1024, 3328], P('rep', 'dp'), parts along dimension 0
- output 5: float32 [8, 1024, 3328], P('rep', 'dp'), parts along dimension 0
- output 6: float32 [8, 3328, 1024], P('rep', 'dp'), parts along dimension 0
- output 7: float32 [8, 1024, 3328], P('rep', 'dp'), parts along dimension 0
- output 8: float32 [8, 1024, 3328], P('rep', 'dp'), parts along dimension 0
- output 9: float32 [8, 3328, 1024], P('rep', 'dp'), parts along dimension 0
There are 4 independent parts. A program takes and returns all parts, laid end to end along the dimension named above; an argument that names none is the same for every part.
All inputs are finite; a program needn't handle non-finite values.
Results may differ from a plain program's by a relative error of at most 0.022.
Values are sent between devices in bfloat16 or wider.
A program may use at most 2 GiB of HBM per device.

v0:
```python
import jax
import jax.numpy as jnp
from jax import lax
from jax.sharding import PartitionSpec as P


def adamw(w, m, v, g):
    m = 0.9 * m + 0.1 * g
    v = 0.95 * v + 0.05 * g * g
    step = m * lax.rsqrt(v + 1e-8) + 0.1 * w
    return (w - 0.02 * step).astype(jnp.bfloat16), m, v


def clipped(gradients, sum_of_squares, count):
    factor = jnp.minimum(1.0, 0.5 * lax.rsqrt(sum_of_squares / count + 1e-30))
    return [g * factor for g in gradients]


def solution(mesh):
    def step(*arrays):
        terms, weights, m, v = (arrays[i : i + 3] for i in (0, 3, 6, 9))
        gradients = [lax.psum_scatter(t[0], "dp", scatter_dimension=1, tiled=True).astype(jnp.float32) for t in terms]
        squares = lax.psum(sum(jnp.sum(g * g) for g in gradients), "dp")
        gradients = clipped(gradients, squares, lax.psum(1, "dp") * sum(g.size for g in gradients))
        me = lax.axis_index("dp")
        own = [lax.dynamic_slice_in_dim(w, me * one.shape[1], one.shape[1], 1).astype(jnp.float32) for w, one in zip(weights, m, strict=True)]
        new = [adamw(w, m, v, g) for w, m, v, g in zip(own, m, v, gradients, strict=True)]
        whole = [lax.all_gather(one[0], "dp", axis=1, tiled=True) for one in new]
        return (*whole, *(one[1] for one in new), *(one[2] for one in new))

    all_of, cut = P(None, None, None), P(None, "dp", None)
    return jax.shard_map(
        step,
        mesh=mesh,
        in_specs=(P(("rep", "dp"), None, None, None),) * 3 + (all_of,) * 3 + (cut,) * 6,
        out_specs=(P("rep", None, None),) * 3 + (P("rep", "dp", None),) * 6,
        check_vma=False,
    )
```

profile of v0, /device:TPU:0, one launch (start us, length us, event | category | flops | bytes accessed | tf_op | source)
XLA Modules:
  0.0 866.2 jit_solution(17228638647229042182)
XLA Ops:
  7.2 0.0 reduce-scatter.4.cloned.1.call-start
  7.2 0.7 reduce-scatter.4.cloned.1.call-update
  7.9 0.0 reduce-scatter.6.cloned.1.call-start
  8.0 0.7 reduce-scatter.6.cloned.1.call-update
  8.7 0.0 reduce-scatter.8.cloned.1.call-start
  8.7 0.7 reduce-scatter.8.cloned.1.call-update
  9.4 0.0 all-gather.8.cloned.1.call-start
  9.4 142.5 %reduce-scatter.4.cloned.1.call-done = bf16[2,128,3328]{2,1,0:T(8,128)(2,1)} async-done(((bf16[2,1024,3328]{2,1,0:T(8,128)(2,1)}), bf16[2,128,3328]{2,1,0:T(8,128)(2,1)}) %reduce-scatter.4.cloned.1.call-update) | async-done | bytes 1703952 | tf_op jit(solution)/shard_map/reduce_scatter | solution.py:22
  151.9 2.9 fusion.9
  154.9 137.0 %reduce-scatter.6.cloned.1.call-done = bf16[2,128,3328]{2,1,0:T(8,128)(2,1)} async-done(((bf16[2,1024,3328]{2,1,0:T(8,128)(2,1)}), bf16[2,128,3328]{2,1,0:T(8,128)(2,1)}) %reduce-scatter.6.cloned.1.call-update) | async-done | bytes 1703952 | tf_op jit(solution)/shard_map/reduce_scatter | solution.py:22
  291.8 2.9 fusion.10
  296.1 135.7 %reduce-scatter.8.cloned.1.call-done = bf16[2,416,1024]{2,1,0:T(8,128)(2,1)} async-done(((bf16[2,3328,1024]{2,1,0:T(8,128)(2,1)}), bf16[2,416,1024]{2,1,0:T(8,128)(2,1)}) %reduce-scatter.8.cloned.1.call-update) | async-done | bytes 1703952 | tf_op jit(solution)/shard_map/reduce_scatter | solution.py:22
  431.7 2.9 fusion.11
  435.3 14.3 %psum.7 = f32[]{:T(128)} all-reduce(f32[]{:T(128)S(6)} %add.65), channel_id=1, replica_groups=mesh['rep'=4,'dp'=8] {'dp'}, use_global_device_ids=true, to_apply=%region_6.0 | all-reduce | flops 1 | bytes 8 | tf_op jit(solution)/shard_map/psum | solution.py:23
  450.4 0.0 copy-start.2
  450.4 6.7 fusion.17
  457.1 0.0 all-gather.8.cloned.1.call-update
  457.1 0.0 all-gather.4.cloned.1.call-start
  457.1 0.0 copy-done.2
  457.2 6.1 fusion.8
  463.3 0.0 all-gather.4.cloned.1.call-update
  463.3 0.0 all-gather.6.cloned.1.call-start
  463.4 6.0 fusion.14
  469.4 0.0 all-gather.6.cloned.1.call-update
  469.4 111.1 %all-gather.8.cloned.1.call-done = bf16[2,3328,1024]{2,1,0:T(8,128)(2,1)} async-done(((bf16[2,416,1024]{2,1,0:T(8,128)(2,1)}), bf16[2,3328,1024]{2,1,0:T(8,128)(2,1)}) %all-gather.8.cloned.1.call-update) | async-done | bytes 13631504 | tf_op jit(solution)/shard_map/all_gather | solution.py:28
  580.5 125.8 %all-gather.4.cloned.1.call-done = bf16[2,1024,3328]{2,1,0:T(8,128)(2,1)} async-done(((bf16[2,128,3328]{2,1,0:T(8,128)(2,1)}), bf16[2,1024,3328]{2,1,0:T(8,128)(2,1)}) %all-gather.4.cloned.1.call-update) | async-done | bytes 13631504 | tf_op jit(solution)/shard_map/all_gather | solution.py:28
  706.3 125.8 %all-gather.6.cloned.1.call-done = bf16[2,1024,3328]{2,1,0:T(8,128)(2,1)} async-done(((bf16[2,128,3328]{2,1,0:T(8,128)(2,1)}), bf16[2,1024,3328]{2,1,0:T(8,128)(2,1)}) %all-gather.6.cloned.1.call-update) | async-done | bytes 13631504 | tf_op jit(solution)/shard_map/all_gather | solution.py:28
  832.1 15.1 %copy.24 = bf16[2,1024,3328]{2,1,0:T(8,128)(2,1)} copy(bf16[2,1024,3328]{2,1,0:T(8,128)(2,1)} %all-gather.4.cloned.1.call-done) | data formatting | bytes 27262976
  847.2 0.0 copy-done
  847.2 6.6 copy.25
  853.7 0.5 slice-done.3
  854.2 5.1 copy.26
  (11 shorter events, 0.0 us)
Async XLA Ops:
  7.2 144.7 %reduce-scatter.4.cloned.1.call-start = ((), (), s32[]{:S(2)}) async-start(), calls=%async_computation.3 | async-start | bytes 15335424 | tf_op jit(solution)/shard_map/reduce_scatter | solution.py:22
  7.9 283.9 %reduce-scatter.6.cloned.1.call-start = ((), (), s32[]{:S(2)}) async-start(), calls=%async_computation.4 | async-start | bytes 15335424 | tf_op jit(solution)/shard_map/reduce_scatter | solution.py:22
  8.7 423.1 %reduce-scatter.8.cloned.1.call-start = ((), (), s32[]{:S(2)}) async-start(), calls=%async_computation.5 | async-start | bytes 15335424 | tf_op jit(solution)/shard_map/reduce_scatter | solution.py:22
  9.4 571.1 %all-gather.8.cloned.1.call-start = ((), (), s32[]{:S(2)}) async-start(), calls=%async_computation.8 | async-start | bytes 15335424 | tf_op jit(solution)/shard_map/all_gather | solution.py:28
  450.4 6.8 copy-start.2
  457.1 249.2 %all-gather.4.cloned.1.call-start = ((), (), s32[]{:S(2)}) async-start(), calls=%async_computation.6 | async-start | bytes 15335424 | tf_op jit(solution)/shard_map/all_gather | solution.py:28
  457.2 6.2 copy-start.1
  463.3 368.8 %all-gather.6.cloned.1.call-start = ((), (), s32[]{:S(2)}) async-start(), calls=%async_computation.7 | async-start | bytes 15335424 | tf_op jit(solution)/shard_map/all_gather | solution.py:28
  832.1 15.1 %copy-start = (bf16[2,1024,3328]{2,1,0:T(8,128)(2,1)S(1)}, bf16[2,1024,3328]{2,1,0:T(8,128)(2,1)}, u32[]{:S(2)}) copy-start(bf16[2,1024,3328]{2,1,0:T(8,128)(2,1)} %all-gather.6.cloned.1.call-done) | copy-start | bytes 40894468
  832.1 21.6 %slice-start = ((s8[13631488]{0:T(1024)(128)(4,1)}), s8[4194304]{0:T(1024)(128)(4,1)S(1)}, s32[]{:S(2)}) async-start(s8[13631488]{0:T(1024)(128)(4,1)} %bitcast.6), calls=%async_computation.9 | async-start | bytes 8388608
  832.1 21.6 %slice-start.1 = ((s8[13631488]{0:T(1024)(128)(4,1)}), s8[4194304]{0:T(1024)(128)(4,1)S(1)}, s32[]{:S(2)}) async-start(s8[13631488]{0:T(1024)(128)(4,1)} %bitcast.6), calls=%async_computation.10 | async-start | bytes 8388608
  847.2 6.6 slice-start.2
  847.2 7.1 slice-start.3
Sparse Core Ops, SparseCore 0:
  10.3 141.5 reduce-scatter.3
  154.2 137.5 reduce-scatter.5
  294.1 137.5 reduce-scatter.7
  457.2 123.2 all-gather.7
  582.6 123.7 all-gather.3
  708.3 123.7 all-gather.5
where the time goes:
time: 866 us
  waiting for transfers between devices  780 us (90%)
  other arithmetic  27.6 us (3%)
  local copies, waits for them, and re-layouts  27.3 us (3%)
  between operations  16.8 us (2%)
  blocking collectives  14.3 us (2%)
    reduce_scatter x3, waiting for transfers between devices, step(): lax.psum_scatter(t[0], 'dp', scatter_dimension=1, tiled=True)  415 us
    all_gather x3, waiting for transfers between devices, step(): whole = [lax.all_gather(one[0], 'dp', axis=1, tiled=True) for one in new]  363 us
    unnamed x17, local copies, waits for them, and re-layouts  27.3 us
    convert_element_type x3, other arithmetic, adamw(): return ((w - 0.02 * step).astype(jnp.bfloat16), m, v)  18.8 us
  transfers between devices with their start and end apart: 6, of which 6 were waited for; matrix products, arithmetic and copies ran while one was open for 2% of the time, Pallas kernels for 0%

commit v1 on v0

v1 whole, which is shorter than its diff:
```python
import functools

import jax
import jax.numpy as jnp
from jax import lax
from jax.experimental import pallas as pl
from jax.experimental.pallas import tpu as pltpu
from jax.sharding import PartitionSpec as P

F32, BF16 = jnp.float32, jnp.bfloat16
HALVES = 2
CHUNKS = 4
GROUP = 8
ROWS = 16


def kernel(count, *refs):
    g, w, m, v = refs[0:3], refs[3:6], refs[6:9], refs[9:12]
    t, gout, fout = refs[12:15], refs[15:18], refs[18]
    x, ein, iin = refs[19:22], refs[22:25], refs[25:28]
    inb, outr, outl = refs[28:30], refs[30:32], refs[32:34]
    mb, vb, wb = refs[34:36], refs[36:38], refs[38:40]
    gv, wn = refs[40:43], refs[43:46]
    nb, fbuf = refs[46:48]
    (ld, osr, osl, xs, xr, er, ir, up, ns, nr, ar, pr, so, si, sp, sl, gs) = refs[48:]

    me = lax.axis_index("dp")
    z, k = me // 2, me % 2
    h = z // 2
    is_end = (z % 3) == 0
    inner, outer = 2 * (z + 1 - 2 * h) + k, 2 * (z - 1 + 2 * h) + k
    partner = 2 * z + 1 - k
    kind = (0, 0, 1)
    rows_of = [r.shape[1] for r in m]
    half_of = [r // HALVES for r in rows_of]

    def chip(J):
        return J + h * (3 - 2 * J)

    def at_layer(q):
        return q // HALVES, q % HALVES

    def full(ref, a, J, parity, q):
        l, s = at_layer(q)
        start = pl.multiple_of((2 * chip(J) + parity) * rows_of[a] + s * half_of[a], 16)
        return ref.at[l, pl.ds(start, half_of[a]), :]

    def part(ref, a, q):
        l, s = at_layer(q)
        return ref.at[l, pl.ds(pl.multiple_of(s * half_of[a], 16), half_of[a]), :]

    def remote(src, dst, send, recv, to):
        return pltpu.make_async_remote_copy(src, dst, send, recv, device_id={"dp": to}, device_id_type=pl.DeviceIdType.MESH)

    barrier = pltpu.get_barrier_semaphore()
    for d in range(1, GROUP):
        pl.semaphore_signal(barrier, inc=1, device_id={"dp": (me + d) % GROUP}, device_id_type=pl.DeviceIdType.MESH)
    pl.semaphore_wait(barrier, GROUP - 1)

    def swap(J, a, l):
        start = pl.multiple_of((2 * chip(J) + 1 - k) * rows_of[a], 16)
        return remote(g[a].at[0, l, pl.ds(start, rows_of[a]), :], x[a].at[J, l], xs.at[J * 6 + a * 2 + l], xr.at[J * 6 + a * 2 + l], partner)

    for J in (3, 0, 2, 1):
        for a in range(3):
            for l in range(2):
                swap(J, a, l).start()

    def moments(a, q):
        slot, c = q % 2, kind[a]
        return (
            pltpu.make_async_copy(part(m[a], a, q), mb[c].at[slot], up.at[slot]),
            pltpu.make_async_copy(part(v[a], a, q), vb[c].at[slot], up.at[2 + slot]),
            pltpu.make_async_copy(full(w[a], a, 0 * q + own_J, k, q), wb[c].at[slot], up.at[4 + slot]),
        )

    own_J = jnp.where(is_end, 0, 1)
    for copy in moments(0, 0):
        copy.start()

    def load(a, J, q, more):
        l, s = at_layer(q)

        @pl.when(s == 0)
        def _():
            remote(x[a].at[J, l], x[a].at[J, l], xs.at[J * 6 + a * 2 + l], xr.at[J * 6 + a * 2 + l], partner).wait_recv()

        sources = [full(g[a].at[0], a, J, k, q), part(x[a].at[J], a, q), *more]
        copies = [pltpu.make_async_copy(src, inb[kind[a]].at[i], ld.at[i]) for i, src in enumerate(sources)]
        for copy in copies:
            copy.start()
        for copy in copies:
            copy.wait()
        return len(copies)

    def total(a, n, r):
        here = pl.ds(pl.multiple_of(r * ROWS, ROWS), ROWS)
        so_far = inb[kind[a]][0, here, :].astype(F32)
        for i in range(1, n):
            so_far = so_far + inb[kind[a]][i, here, :].astype(F32)
        return so_far.astype(BF16)

    def send(a, J, q, more, out, sem, dst, recv, to, first):
        c = kind[a]
        copy = remote(out[c].at[q], dst, sem.at[c * CHUNKS + q], recv, to)
        n = load(a, J, q, more)
        if not first:
            copy.wait_send()

        def row(r, _):
            out[c][q, pl.ds(pl.multiple_of(r * ROWS, ROWS), ROWS), :] = total(a, n, r)
            return 0

        lax.fori_loop(0, half_of[a] // ROWS, row, 0)
        copy.start()

    def final(a, J, q, more, acc):
        l, s = at_layer(q)
        n = load(a, J, q, more)

        def row(r, acc):
            one = total(a, n, r)
            gv[a][l, pl.ds(pl.multiple_of(s * half_of[a] + r * ROWS, ROWS), ROWS), :] = one
            one = one.astype(F32)
            one = one * one
            for i in range(one.shape[1] // 128):
                acc = acc + one[:, i * 128 : (i + 1) * 128]
            return acc

        return lax.fori_loop(0, half_of[a] // ROWS, row, acc)

    def from_end(a, p, q):
        i = p * 12 + a * CHUNKS + q
        return remote(part(ein[a].at[p], a, q), part(ein[a].at[p], a, q), osr.at[0], er.at[i], outer)

    def from_inner(a, p, q):
        i = p * 12 + a * CHUNKS + q
        return remote(part(iin[a].at[p], a, q), part(iin[a].at[p], a, q), osr.at[0], ir.at[i], inner)

    def loop(body):
        lax.fori_loop(0, CHUNKS, lambda q, _: (body(q), 0)[1], 0)

    zero = jnp.zeros((ROWS, 128), F32)

    def drain(out, sem):
        for a in (1, 2):
            for q in range(CHUNKS):
                remote(out[kind[a]].at[q], out[kind[a]].at[q], sem.at[kind[a] * CHUNKS + q], sem.at[kind[a] * CHUNKS + q], inner).wait_send()

    @pl.when(is_end)
    def _():
        acc = zero
        for p in range(3):
            for a in range(3):

                def both(q, acc, p=p, a=a):
                    i = p * 12 + a * CHUNKS + q
                    send(a, 3 - p, q, [], outr, osr, part(ein[a].at[p], a, q), er.at[i], inner, p == 0 and a != 1)
                    if p == 1:
                        from_inner(a, 0, q).wait_recv()
                        acc = final(a, 0, q, [part(iin[a].at[0], a, q)], acc)
                    return acc

                acc = lax.fori_loop(0, CHUNKS, both, acc)
        fbuf[...] = acc[:8] + acc[8:]
        drain(outr, osr)

    @pl.when(jnp.logical_not(is_end))
    def _():
        def inward(p, a, q):
            from_end(a, p, q).wait_recv()
            i = p * 12 + a * CHUNKS + q
            send(a, 3 - p, q, [part(ein[a].at[p], a, q)], outr, osr, part(iin[a].at[p], a, q), ir.at[i], inner, p == 0 and a != 1)

        def outward(a, q):
            from_inner(a, 0, q).wait_recv()
            send(a, 0, q, [part(iin[a].at[0], a, q)], outl, osl, part(iin[a].at[0], a, q), ir.at[a * CHUNKS + q], outer, a != 1)

        for a in range(4):

            def both(q, a=a):
                if a < 3:
                    inward(0, a, q)
                if a > 0:
                    outward(a - 1, q)

            loop(both)
        for a in range(3):
            loop(functools.partial(inward, 1, a))
        acc = zero
        for a in range(3):

            def last(q, acc, a=a):
                from_inner(a, 1, q).wait_recv()
                from_end(a, 2, q).wait_recv()
                return final(a, 1, q, [part(ein[a].at[2], a, q), part(iin[a].at[1], a, q)], acc)

            acc = lax.fori_loop(0, CHUNKS, last, acc)
        fbuf[...] = acc[:8] + acc[8:]
        drain(outr, osr)
        drain(outl, osl)

    nb[me] = fbuf[...]
    sums = [remote(nb.at[me], nb.at[me], ns.at[d], nr.at[d], (me + d) % GROUP) for d in range(1, GROUP)]
    for copy in sums:
        copy.start()
    for a in range(3):
        pltpu.make_async_copy(gv[a], gout[a], gs.at[a]).start()
    for copy in sums:
        copy.wait()
    squares = nb[0]
    for d in range(1, GROUP):
        squares = squares + nb[d]
    squares = jnp.sum(jnp.sum(squares, axis=0, keepdims=True), axis=1, keepdims=True)
    factor = jnp.minimum(1.0, 0.5 * lax.rsqrt(squares / count + 1e-30))
    fbuf[...] = jnp.broadcast_to(factor, fbuf.shape)
    fout[...] = fbuf[...]

    def give(a, q, J, src, to_inner, to_outer):
        c = a * CHUNKS + q
        dst = full(t[a], a, J, k, q)
        remote(src, dst, sp.at[J * 12 + c], pr.at[J * 12 + c], partner).start()
        if to_inner is not None:
            remote(src, dst, si.at[to_inner[0] * 12 + c], ar.at[to_inner[1] * 12 + c], inner).start()
        if to_outer is not None:
            remote(src, dst, so.at[to_outer * 12 + c], ar.at[to_outer * 12 + c], outer).start()

    for a in range(3):

        def update(q, a=a):
            c, slot = kind[a], q % 2
            l, s = at_layer(q)
            for copy in moments(a, q):
                copy.wait()

            @pl.when(q < CHUNKS - 1)
            def _():
                for copy in moments(a, q + 1):
                    copy.start()

            if a < 2:

                @pl.when(q == CHUNKS - 1)
                def _():
                    for copy in moments(a + 1, q * 0):
                        copy.start()

            def row(r, _):
                here = pl.ds(pl.multiple_of(r * ROWS, ROWS), ROWS)
                there = pl.ds(pl.multiple_of(s * half_of[a] + r * ROWS, ROWS), ROWS)
                one = gv[a][l, there, :].astype(F32) * fbuf[0:1, 0:1]
                m1 = 0.9 * mb[c][slot, here, :] + 0.1 * one
                v1 = 0.95 * vb[c][slot, here, :] + 0.05 * one * one
                old = wb[c][slot, here, :].astype(F32)
                wn[a][l, there, :] = (old - 0.02 * (m1 * lax.rsqrt(v1 + 1e-8) + 0.1 * old)).astype(BF16)
                return 0

            lax.fori_loop(0, half_of[a] // ROWS, row, 0)
            src = part(wn[a], a, q)

            @pl.when(is_end)
            def _():
                give(a, q, 0, src, (0, 2), None)

            @pl.when(jnp.logical_not(is_end))
            def _():
                give(a, q, 1, src, (0, 0), 0)

            pltpu.make_async_copy(src, full(t[a], a, own_J, k, q), sl.at[a * CHUNKS + q]).start()

        loop(update)

    def arrived(a, q, J, slot):
        here = full(t[a], a, J, k, q)
        remote(here, here, sl.at[0], ar.at[slot * 12 + a * CHUNKS + q], inner).wait_recv()

    @pl.when(is_end)
    def _():
        for slot in range(3):
            for a in range(3):

                def on(q, a=a, slot=slot):
                    arrived(a, q, slot + 1, slot)
                    give(a, q, slot + 1, full(t[a], a, slot + 1, k, q), None, None)

                loop(on)

    @pl.when(jnp.logical_not(is_end))
    def _():
        for a in range(3):

            def on(q, a=a):
                arrived(a, q, 2, 0)
                give(a, q, 2, full(t[a], a, 2, k, q), None, 1)
                arrived(a, q, 0, 2)
                give(a, q, 0, full(t[a], a, 0, k, q), (1, 1), None)

            loop(on)
        for a in range(3):

            def on(q, a=a):
                arrived(a, q, 3, 1)
                give(a, q, 3, full(t[a], a, 3, k, q), None, 2)

            loop(on)

    for a in range(3):

        def rest(q, a=a):
            c = a * CHUNKS + q
            for J in range(4):
                mine, theirs = full(t[a], a, J, k, q), full(t[a], a, J, 1 - k, q)
                remote(mine, mine, sp.at[J * 12 + c], pr.at[J * 12 + c], partner).wait_send()
                remote(theirs, theirs, sp.at[J * 12 + c], pr.at[J * 12 + c], partner).wait_recv()
            here = full(t[a], a, own_J, k, q)
            pltpu.make_async_copy(part(wn[a], a, q), here, sl.at[c]).wait()
            remote(here, here, si.at[c], ar.at[c], inner).wait_send()

            @pl.when(jnp.logical_not(is_end))
            def _():
                remote(here, here, si.at[12 + c], ar.at[c], inner).wait_send()
                for n in range(3):
                    remote(here, here, so.at[n * 12 + c], ar.at[c], outer).wait_send()

        loop(rest)
        pltpu.make_async_copy(gv[a], gout[a], gs.at[a]).wait()
        for J in range(4):
            for l in range(2):
                swap(J, a, l).wait_send()


def solution(mesh):
    def step(*arrays):
        terms, weights, m, v = (arrays[i : i + 3] for i in (0, 3, 6, 9))
        blocks = [one.shape for one in m]
        count = GROUP * sum(one.size for one in m)
        pair = (blocks[0], blocks[2])
        chunk = [(one[1] // HALVES, one[2]) for one in pair]
        any_space = pl.BlockSpec(memory_space=pl.ANY)
        out_shape = (
            [jax.ShapeDtypeStruct(one.shape, BF16) for one in weights]
            + [jax.ShapeDtypeStruct(one, BF16) for one in blocks]
            + [jax.ShapeDtypeStruct((8, 128), F32)]
            + [jax.ShapeDtypeStruct((4, *one), BF16) for one in blocks]
            + [jax.ShapeDtypeStruct((3, *one), BF16) for one in blocks]
            + [jax.ShapeDtypeStruct((2, *one), BF16) for one in blocks]
        )
        out_specs = [any_space] * 6 + [pl.BlockSpec(memory_space=pltpu.VMEM)] + [any_space] * 9
        dma = pltpu.SemaphoreType.DMA
        scratch = (
            [pltpu.VMEM((4, *one), BF16) for one in chunk]
            + [pltpu.VMEM((CHUNKS, *one), BF16) for one in chunk]
            + [pltpu.VMEM((CHUNKS, *one), BF16) for one in chunk]
            + [pltpu.VMEM((2, *one), F32) for one in chunk]
            + [pltpu.VMEM((2, *one), F32) for one in chunk]
            + [pltpu.VMEM((2, *one), BF16) for one in chunk]
            + [pltpu.VMEM(one, BF16) for one in blocks]
            + [pltpu.VMEM(one, BF16) for one in blocks]
            + [pltpu.VMEM((GROUP, 8, 128), F32), pltpu.VMEM((8, 128), F32)]
            + [dma((n,)) for n in (4, 8, 8, 24, 24, 36, 24, 6, 8, 8, 36, 48, 36, 24, 48, 12, 3)]
        )
        out = pl.pallas_call(
            functools.partial(kernel, count),
            out_shape=out_shape,
            in_specs=[any_space] * 12,
            out_specs=out_specs,
            scratch_shapes=scratch,
            compiler_params=pltpu.CompilerParams(collective_id=0, has_side_effects=True, vmem_limit_bytes=48 * 2**20),
            name="step",
        )(*arrays)
        whole, sums, factor = out[:3], out[3:6], out[6][0, 0]
        new_m, new_v = [], []
        for one, m1, v1 in zip(sums, m, v, strict=True):
            one = one.astype(F32) * factor
            new_m.append(0.9 * m1 + 0.1 * one)
            new_v.append(0.95 * v1 + 0.05 * one * one)
        return (*whole, *new_m, *new_v)

    all_of, cut = P(None, None, None), P(None, "dp", None)
    return jax.shard_map(
        step,
        mesh=mesh,
        in_specs=(P(("rep", "dp"), None, None, None),) * 3 + (all_of,) * 3 + (cut,) * 6,
        out_specs=(P("rep", None, None),) * 3 + (P("rep", "dp", None),) * 6,
        check_vma=False,
    )
```

time: 866 us -> 723 us (0.83)
  waiting for transfers between devices: 780 us -> 0 us
  Pallas kernels: 0 us -> 678 us
  between operations: 16.8 us -> 0.74 us
  blocking collectives: 14.3 us -> 0 us
  other arithmetic: 27.6 us -> 15.8 us
    pallas_call x0 -> x1, Pallas kernels: none -> 678 us  [step(): pl.pallas_call(functools.partial(kernel, count), out_shape=out_shape, in_...]
    reduce_scatter x3 -> x0, waiting for transfers between devices: 415 us -> none  [step(): lax.psum_scatter(t[0], 'dp', scatter_dimension=1, tiled=True)]
    all_gather x3 -> x0, waiting for transfers between devices: 363 us -> none  [step(): whole = [lax.all_gather(one[0], 'dp', axis=1, tiled=True) for one in new]]
    convert_element_type x3 -> x0, other arithmetic: 18.8 us -> none  [adamw(): return ((w - 0.02 * step).astype(jnp.bfloat16), m, v)]
    add x0 -> x2, other arithmetic: none -> 15.8 us  [step(): new_v.append(0.95 * v1 + 0.05 * one * one)]
    psum x1 -> x0, blocking collectives: 14.3 us -> none  [step(): squares = lax.psum(sum((jnp.sum(g * g) for g in gradients)), 'dp')]
    reduce_sum x3 -> x0, other arithmetic: 8.8 us -> none  [step(): squares = lax.psum(sum((jnp.sum(g * g) for g in gradients)), 'dp')]
    unnamed x17 -> x25, local copies, waits for them, and re-layouts: 27.3 us -> 25.7 us
  transfers between devices with their start and end apart: 6 -> 0, of which waited for: 6 -> 0; matrix products, arithmetic and copies ran while one was open for 2% -> 0% of each run, Pallas kernels for 0% -> 0%
where the time goes in v1:
time: 723 us; the launch traced here: 721 us
  Pallas kernels  678 us (94%)
  local copies, waits for them, and re-layouts  26.3 us (4%)
  other arithmetic  15.8 us (2%)
    pallas_call x1, Pallas kernels, step(): pl.pallas_call(functools.partial(kernel, count), out_shape=out_shape, in_...  678 us
    unnamed x25, local copies, waits for them, and re-layouts  25.7 us
    add x2, other arithmetic, step(): new_v.append(0.95 * v1 + 0.05 * one * one)  15.8 us

profile of v1, /device:TPU:0, one launch (start us, length us, event | category | flops | bytes accessed | tf_op | source)
XLA Modules:
  0.0 721.3 jit_solution(5799385914107507399)
XLA Ops:
  0.6 0.0 copy-start.1
  0.7 0.0 copy-start
  0.7 678.5 %step.1 = (bf16[2,1024,3328]{2,1,0:T(8,128)(2,1)}, bf16[2,1024,3328]{2,1,0:T(8,128)(2,1)}, bf16[2,3328,1024]{2,1,0:T(8,128)(2,1)}, bf16[2,128,3328]{2,1,0:T(8,12...) custom-call(bf16[1,2,1024,3328]{3,2,1,0:T(8,128)(2,1)} %refs_0_.1, ...), custom_call_target="tpu_custom_call" | custom-call | tf_op jit(solution)/shard_map/step/pallas_call | solution.py:362
  679.1 0.5 slice.3
  679.7 0.0 copy-done.1
  679.7 0.0 copy-done
  679.7 0.0 copy-start.2
  679.7 5.4 fusion.2
  685.1 0.0 copy-done.2
  685.1 0.0 slice-start.4
  685.1 0.0 slice-start.5
  685.1 0.0 slice-start.6
  685.1 10.4 %fusion = (f32[2,128,3328]{2,1,0:T(8,128)}, f32[2,128,3328]{2,1,0:T(8,128)}, f32[2,128,3328]{2,1,0:T(8,128)}, f32[2,128,3328]{2,1,0:T(8,128)}) fusion(f32[2,128,3328]{2,1,0:T(8,128)} %refs_9_.1, bf16[2,128,3328]{2,1,0:T(8,128)(2,1)S(1)} %get-tuple-element.19, f32[]{:T(128)} %bitcast, f32[2,128,3328]{2,1,0:T(8,128)S(1)} %copy-done.2, ...), kind=kLoop, calls=%fused_computation.3 | loop fusion | flops 15335424 | bytes 30670852 | tf_op jit(solution)/shard_map/add | solution.py:376
  695.5 0.0 slice-start.7
  695.5 0.0 slice-start
  695.5 0.0 slice-start.1
  695.5 14.2 %copy.24 = bf16[2,1024,3328]{2,1,0:T(8,128)(2,1)} copy(bf16[2,1024,3328]{2,1,0:T(8,128)(2,1)} %get-tuple-element.40) | data formatting | bytes 27262976
  709.7 0.0 slice-done.4
  709.7 0.0 slice-done.5
  709.7 0.0 slice-done.6
  709.7 0.0 slice-done.7
  709.7 0.0 slice-start.2
  709.7 0.0 slice-start.3
  709.7 6.4 copy.25
  716.1 0.0 slice-done
  716.1 0.0 slice-done.1
  716.1 0.0 slice-done.2
  716.1 0.0 slice-done.3
  716.1 5.1 copy.26
  (2 shorter events, 0.0 us)
Async XLA Ops:
  0.6 679.0 %copy-start.1 = (f32[2,416,1024]{2,1,0:T(8,128)S(1)}, f32[2,416,1024]{2,1,0:T(8,128)}, u32[]{:S(2)}) copy-start(f32[2,416,1024]{2,1,0:T(8,128)} %refs_11_.1) | copy-start | bytes 10223620
  0.7 679.0 %copy-start = (f32[2,416,1024]{2,1,0:T(8,128)S(1)}, f32[2,416,1024]{2,1,0:T(8,128)}, u32[]{:S(2)}) copy-start(f32[2,416,1024]{2,1,0:T(8,128)} %refs_8_.1) | copy-start | bytes 10223620
  679.7 5.4 copy-start.2
  685.1 24.6 %slice-start.4 = ((s8[13631488]{0:T(1024)(128)(4,1)}), s8[4194304]{0:T(1024)(128)(4,1)S(1)}, s32[]{:S(2)}) async-start(s8[13631488]{0:T(1024)(128)(4,1)} %bitcast.3), calls=%async_computation.4 | async-start | bytes 8388608
  685.1 24.6 %slice-start.5 = ((s8[13631488]{0:T(1024)(128)(4,1)}), s8[4194304]{0:T(1024)(128)(4,1)S(1)}, s32[]{:S(2)}) async-start(s8[13631488]{0:T(1024)(128)(4,1)} %bitcast.3), calls=%async_computation.5 | async-start | bytes 8388608
  685.1 24.6 %slice-start.6 = ((s8[13631488]{0:T(1024)(128)(4,1)}), s8[1048576]{0:T(1024)(128)(4,1)S(1)}, s32[]{:S(2)}) async-start(s8[13631488]{0:T(1024)(128)(4,1)} %bitcast.3), calls=%async_computation.6 | async-start | bytes 2097152
  695.5 14.2 %slice-start.7 = ((s8[13631488]{0:T(1024)(128)(4,1)}), s8[4194304]{0:T(1024)(128)(4,1)S(1)}, s32[]{:S(2)}) async-start(s8[13631488]{0:T(1024)(128)(4,1)} %bitcast.3), calls=%async_computation.7 | async-start | bytes 8388608
  695.5 20.6 %slice-start = ((s8[13631488]{0:T(1024)(128)(4,1)}), s8[4194304]{0:T(1024)(128)(4,1)S(1)}, s32[]{:S(2)}) async-start(s8[13631488]{0:T(1024)(128)(4,1)} %bitcast.1), calls=%async_computation | async-start | bytes 8388608
  695.5 20.6 %slice-start.1 = ((s8[13631488]{0:T(1024)(128)(4,1)}), s8[4194304]{0:T(1024)(128)(4,1)S(1)}, s32[]{:S(2)}) async-start(s8[13631488]{0:T(1024)(128)(4,1)} %bitcast.1), calls=%async_computation.1 | async-start | bytes 8388608
  709.7 6.4 slice-start.2
  709.7 6.4 slice-start.3

commit v2 on v1

v2 whole, which is shorter than its diff:
```python
import functools

import jax
import jax.numpy as jnp
from jax import lax
from jax.experimental import pallas as pl
from jax.experimental.pallas import tpu as pltpu
from jax.sharding import PartitionSpec as P

F32, BF16 = jnp.float32, jnp.bfloat16
HALVES = 2
CHUNKS = 4
GROUP = 8
LENT = 0
ORDER = (1, 2, 0)
OUTR, OUTL = 4, 6
LIMIT = 5 * 2**20
ROWS = 16


def kernel(count, *refs):
    g, w, m, v = refs[0:3], refs[3:6], refs[6:9], refs[9:12]
    t, nm, nv = refs[12:15], refs[15:18], refs[18:21]
    x, ein, iin = refs[21:24], refs[24:27], refs[27:30]
    xm, xv = refs[30:32]
    wb, lm, lv = refs[32:34], refs[34], refs[35]
    nb, fbuf = refs[36:38]
    (ld, osr, osl, xs, xr, er, ir, up, ns, nr, ar, pr, so, si, sp, ms, mr, hs, hr, mo) = refs[38:]

    me = lax.axis_index("dp")
    z, k = me // 2, me % 2
    h = z // 2
    is_end = (z % 3) == 0
    inner, outer = 2 * (z + 1 - 2 * h) + k, 2 * (z - 1 + 2 * h) + k
    partner = 2 * z + 1 - k
    kind = (0, 0, 1)
    rows_of = [r.shape[1] for r in m]
    half_of = [r // HALVES for r in rows_of]

    def chip(J):
        return J + h * (3 - 2 * J)

    def at_layer(q):
        return q // HALVES, q % HALVES

    def full(ref, a, J, parity, q):
        l, s = at_layer(q)
        start = pl.multiple_of((2 * chip(J) + parity) * rows_of[a] + s * half_of[a], 16)
        return ref.at[l, pl.ds(start, half_of[a]), :]

    def part(ref, a, q):
        l, s = at_layer(q)
        return ref.at[l, pl.ds(pl.multiple_of(s * half_of[a], 16), half_of[a]), :]

    def slot_start(c, i):
        rows, half = rows_of[c + 1], half_of[c + 1]
        return pl.multiple_of(((2 * z + k) * rows + rows + i * half) % (GROUP * rows), 16)

    def staged(c, i):
        return t[c + 1].at[0, pl.ds(slot_start(c, i), half_of[c + 1]), :]

    def staged_rows(c, i, r):
        return 0, pl.ds(pl.multiple_of(slot_start(c, i) + r * ROWS, ROWS), ROWS), slice(None)

    def remote(src, dst, send, recv, to):
        return pltpu.make_async_remote_copy(src, dst, send, recv, device_id={"dp": to}, device_id_type=pl.DeviceIdType.MESH)

    barrier = pltpu.get_barrier_semaphore()
    for d in range(1, GROUP):
        pl.semaphore_signal(barrier, inc=1, device_id={"dp": (me + d) % GROUP}, device_id_type=pl.DeviceIdType.MESH)
    pl.semaphore_wait(barrier, GROUP - 1)

    def swap(J, a, l):
        start = pl.multiple_of((2 * chip(J) + 1 - k) * rows_of[a], 16)
        return remote(g[a].at[0, l, pl.ds(start, rows_of[a]), :], x[a].at[J, l], xs.at[J * 6 + a * 2 + l], xr.at[J * 6 + a * 2 + l], partner)

    def give_terms(J, weights=(0, 1, 2)):
        for a in weights:
            for l in range(2):
                swap(J, a, l).start()

    give_terms(3, (0,))

    own_J = jnp.where(is_end, 0, 1)

    def old_weight(a, q, J=own_J):
        return pltpu.make_async_copy(full(w[a], a, J, k, q), wb[kind[a]].at[q % 2], up.at[q % 2])

    old_weight(ORDER[0], 0).start()

    def moments(a):
        return pltpu.make_async_copy(m[a], nm[a], mo.at[a]), pltpu.make_async_copy(v[a], nv[a], mo.at[3 + a])

    def load(a, J, q, more):
        l, s = at_layer(q)

        @pl.when(s == 0)
        def _():
            remote(x[a].at[J, l], x[a].at[J, l], xs.at[J * 6 + a * 2 + l], xr.at[J * 6 + a * 2 + l], partner).wait_recv()

        sources = [full(g[a].at[0], a, J, k, q), part(x[a].at[J], a, q), *more]
        copies = [pltpu.make_async_copy(src, staged(kind[a], i), ld.at[i]) for i, src in enumerate(sources)]
        for copy in copies:
            copy.start()
        for copy in copies:
            copy.wait()
        return len(copies)

    def total(a, n, r):
        so_far = t[kind[a] + 1][staged_rows(kind[a], 0, r)].astype(F32)
        for i in range(1, n):
            so_far = so_far + t[kind[a] + 1][staged_rows(kind[a], i, r)].astype(F32)
        return so_far.astype(BF16)

    def send(a, J, q, more, out, sem, dst, recv, to, first):
        c, slot = kind[a], q % 2
        copy = remote(staged(c, out + slot), dst, sem.at[c * 2 + slot], recv, to)
        n = load(a, J, q, more)
        if first:

            @pl.when(q >= 2)
            def _():
                copy.wait_send()
        else:
            copy.wait_send()

        def row(r, _):
            t[c + 1][staged_rows(c, out + slot, r)] = total(a, n, r)
            return 0

        lax.fori_loop(0, half_of[a] // ROWS, row, 0)
        copy.start()

    def final(a, J, q, more, acc):
        l, s = at_layer(q)
        n = load(a, J, q, more)

        def row(r, acc):
            one = total(a, n, r)
            t[a][l, pl.ds(pl.multiple_of((2 * z + k) * rows_of[a] + s * half_of[a] + r * ROWS, ROWS), ROWS), :] = one
            one = one.astype(F32)
            one = one * one
            for i in range(one.shape[1] // 128):
                acc = acc + one[:, i * 128 : (i + 1) * 128]
            return acc

        return lax.fori_loop(0, half_of[a] // ROWS, row, acc)

    def more_terms(p, a, q):
        if p == 0 and a == 0:

            @pl.when(q == 1)
            def _():
                give_terms(3, (1, 2))

    def from_end(a, p, q):
        i = p * 12 + a * CHUNKS + q
        return remote(part(ein[a].at[p], a, q), part(ein[a].at[p], a, q), osr.at[0], er.at[i], outer)

    def from_inner(a, p, q):
        i = p * 12 + a * CHUNKS + q
        return remote(part(iin[a].at[p], a, q), part(iin[a].at[p], a, q), osr.at[0], ir.at[i], inner)

    def lend(l):
        return (
            remote(m[LENT].at[l], xm.at[l], ms.at[l], mr.at[l], outer),
            remote(v[LENT].at[l], xv.at[l], ms.at[2 + l], mr.at[2 + l], outer),
        )

    def lend_sum(q):
        here = full(t[LENT], LENT, 1, k, q)
        return remote(here, here, hs.at[q], hr.at[q], outer)

    def loop(body):
        lax.fori_loop(0, CHUNKS, lambda q, _: (body(q), 0)[1], 0)

    zero = jnp.zeros((ROWS, 128), F32)

    def drain(out, sem):
        for a in (1, 2):
            for slot in range(2):
                one, on = staged(kind[a], out + slot), sem.at[kind[a] * 2 + slot]
                remote(one, one, on, on, inner).wait_send()

    @pl.when(is_end)
    def _():
        acc = zero
        for p in range(3):
            for a in range(3):

                if p == 0 and a > 0:
                    give_terms((0, 2)[a - 1])
                if p == 1 and a == 0:
                    give_terms(1)
                if p == 1:
                    for copy in moments(a):
                        copy.start()

                def both(q, acc, p=p, a=a):
                    i = p * 12 + a * CHUNKS + q
                    more_terms(p, a, q)
                    send(a, 3 - p, q, [], OUTR, osr, part(ein[a].at[p], a, q), er.at[i], inner, p == 0 and a != 1)
                    if p == 1:
                        from_inner(a, 0, q).wait_recv()
                        acc = final(a, 0, q, [part(iin[a].at[0], a, q)], acc)
                    return acc

                acc = lax.fori_loop(0, CHUNKS, both, acc)
        fbuf[...] = acc[:8] + acc[8:]
        drain(OUTR, osr)

    @pl.when(jnp.logical_not(is_end))
    def _():
        def inward(p, a, q):
            from_end(a, p, q).wait_recv()
            i = p * 12 + a * CHUNKS + q
            send(a, 3 - p, q, [part(ein[a].at[p], a, q)], OUTR, osr, part(iin[a].at[p], a, q), ir.at[i], inner, p == 0 and a != 1)

        def outward(a, q):
            from_inner(a, 0, q).wait_recv()
            send(a, 0, q, [part(iin[a].at[0], a, q)], OUTL, osl, part(iin[a].at[0], a, q), ir.at[a * CHUNKS + q], outer, a != 1)

        for copy in lend(0):
            copy.start()
        for a in range(4):
            if a > 0:
                give_terms((0, 2, 1)[a - 1])

            def both(q, a=a):
                more_terms(0, a, q)
                if a < 3:
                    inward(0, a, q)
                if a > 0:
                    outward(a - 1, q)

            loop(both)
        for copy in lend(1):
            copy.start()
        for a in range(3):
            for copy in moments(a):
                copy.start()
        for a in range(3):
            loop(functools.partial(inward, 1, a))
        acc = zero
        for a in range(3):

            def last(q, acc, a=a):
                from_inner(a, 1, q).wait_recv()
                from_end(a, 2, q).wait_recv()
                acc = final(a, 1, q, [part(ein[a].at[2], a, q), part(iin[a].at[1], a, q)], acc)
                if a == LENT:
                    lend_sum(q).start()
                return acc

            acc = lax.fori_loop(0, CHUNKS, last, acc)
        fbuf[...] = acc[:8] + acc[8:]
        drain(OUTR, osr)
        drain(OUTL, osl)

    nb[me] = fbuf[...]
    sums = [remote(nb.at[me], nb.at[me], ns.at[d], nr.at[d], (me + d) % GROUP) for d in range(1, GROUP)]
    for copy in sums:
        copy.start()
    for copy in sums:
        copy.wait()

    squares = nb[0]
    for d in range(1, GROUP):
        squares = squares + nb[d]
    squares = jnp.sum(jnp.sum(squares, axis=0, keepdims=True), axis=1, keepdims=True)
    factor = jnp.minimum(1.0, 0.5 * lax.rsqrt(squares / count + 1e-30))
    fbuf[...] = jnp.broadcast_to(factor, fbuf.shape)

    def give(a, q, J, src, to_inner, to_outer):
        c = a * CHUNKS + q
        dst = full(t[a], a, J, k, q)
        remote(src, dst, sp.at[J * 12 + c], pr.at[J * 12 + c], partner).start()
        if to_inner is not None:
            remote(src, dst, si.at[to_inner[0] * 12 + c], ar.at[to_inner[1] * 12 + c], inner).start()
        if to_outer is not None:
            remote(src, dst, so.at[to_outer * 12 + c], ar.at[to_outer * 12 + c], outer).start()

    def stepped(a, q, J, mv, at_row):
        c, slot = kind[a], q % 2
        l, s = at_layer(q)
        start = (2 * chip(J) + k) * rows_of[a] + s * half_of[a]

        def row(r, _):
            here = pl.ds(pl.multiple_of(r * ROWS, ROWS), ROWS)
            there = pl.ds(pl.multiple_of(start + r * ROWS, ROWS), ROWS)
            those = pl.ds(pl.multiple_of(at_row + r * ROWS, ROWS), ROWS)
            (m_in, v_in), layer = mv, l if len(mv[0].shape) == 3 else None
            at = (those, slice(None)) if layer is None else (layer, those, slice(None))
            one = t[a][l, there, :].astype(F32) * fbuf[0:1, 0:1]
            m1 = 0.9 * m_in[at] + 0.1 * one
            v1 = 0.95 * v_in[at] + 0.05 * one * one
            if layer is not None:
                m_in[at] = m1
                v_in[at] = v1
            old = wb[c][slot, here, :].astype(F32)
            t[a][l, there, :] = (old - 0.02 * (m1 * lax.rsqrt(v1 + 1e-8) + 0.1 * old)).astype(BF16)
            return 0

        lax.fori_loop(0, half_of[a] // ROWS, row, 0)

    for n, a in enumerate(ORDER):
        if a == LENT:

            @pl.when(jnp.logical_not(is_end))
            def _():
                for q in range(CHUNKS):
                    lend_sum(q).wait_send()

        for copy in moments(a):
            copy.wait()

        def update(q, n=n, a=a):
            old_weight(a, q).wait()

            @pl.when(q < CHUNKS - 1)
            def _():
                old_weight(a, q + 1).start()

            if n < 2:

                @pl.when(q == CHUNKS - 1)
                def _():
                    old_weight(ORDER[n + 1], q * 0).start()

            stepped(a, q, own_J, (nm[a], nv[a]), at_layer(q)[1] * half_of[a])
            src = full(t[a], a, own_J, k, q)

            @pl.when(is_end)
            def _():
                give(a, q, 0, src, (0, 2), None)

            @pl.when(jnp.logical_not(is_end))
            def _():
                give(a, q, 1, src, (0, 0), None if a == LENT else 0)

        loop(update)

    @pl.when(is_end)
    def _():
        def lent(q):
            a = LENT
            lend_sum(q).wait_recv()

            @pl.when(q % HALVES == 0)
            def _():
                for copy in lend(q // HALVES):
                    copy.wait_recv()

            copies = (
                pltpu.make_async_copy(part(xm, a, q), lm, up.at[2]),
                pltpu.make_async_copy(part(xv, a, q), lv, up.at[3]),
                old_weight(a, q, 1),
            )
            for copy in copies:
                copy.start()
            for copy in copies:
                copy.wait()
            stepped(a, q, 1, (lm, lv), 0)
            give(a, q, 1, full(t[a], a, 1, k, q), None, None)

        loop(lent)

    def arrived(a, q, J, slot):
        here = full(t[a], a, J, k, q)
        remote(here, here, sp.at[0], ar.at[slot * 12 + a * CHUNKS + q], inner).wait_recv()

    @pl.when(is_end)
    def _():
        for slot in range(3):
            for a in ORDER:
                if slot == 0 and a == LENT:
                    continue

                def on(q, a=a, slot=slot):
                    arrived(a, q, slot + 1, slot)
                    give(a, q, slot + 1, full(t[a], a, slot + 1, k, q), None, None)

                loop(on)

    @pl.when(jnp.logical_not(is_end))
    def _():
        for a in ORDER:

            def on(q, a=a):
                arrived(a, q, 2, 0)
                give(a, q, 2, full(t[a], a, 2, k, q), None, 1)
                arrived(a, q, 0, 2)
                give(a, q, 0, full(t[a], a, 0, k, q), (1, 1), None)

            loop(on)
        for a in ORDER:

            def on(q, a=a):
                arrived(a, q, 3, 1)
                give(a, q, 3, full(t[a], a, 3, k, q), None, 2)

            loop(on)

    for a in range(3):

        def rest(q, a=a):
            c = a * CHUNKS + q
            for J in range(4):
                mine, theirs = full(t[a], a, J, k, q), full(t[a], a, J, 1 - k, q)
                remote(mine, mine, sp.at[J * 12 + c], pr.at[J * 12 + c], partner).wait_send()
                remote(theirs, theirs, sp.at[J * 12 + c], pr.at[J * 12 + c], partner).wait_recv()
            here = full(t[a], a, own_J, k, q)
            remote(here, here, si.at[c], ar.at[c], inner).wait_send()

            @pl.when(jnp.logical_not(is_end))
            def _():
                remote(here, here, si.at[12 + c], ar.at[c], inner).wait_send()
                for n in range(1 if a == LENT else 0, 3):
                    remote(here, here, so.at[n * 12 + c], ar.at[c], outer).wait_send()

        loop(rest)
        for J in range(4):
            for l in range(2):
                swap(J, a, l).wait_send()

    @pl.when(jnp.logical_not(is_end))
    def _():
        for l in range(2):
            for copy in lend(l):
                copy.wait_send()


def finish(*refs):
    n = (len(refs) - 1) // 2
    copies = [
        pltpu.make_async_copy(refs[i].at[l], refs[n + i].at[l], refs[-1].at[i, l]) for i in range(n) for l in range(refs[i].shape[0])
    ]
    for copy in copies:
        copy.start()
    for copy in copies:
        copy.wait()


def solution(mesh):
    def step(*arrays):
        terms, weights, m, v = (arrays[i : i + 3] for i in (0, 3, 6, 9))
        blocks = [one.shape for one in m]
        count = GROUP * sum(one.size for one in m)
        pair = (blocks[0], blocks[2])
        chunk = [(one[1] // HALVES, one[2]) for one in pair]
        results = [(one.shape, BF16) for one in weights] + [(one, F32) for one in blocks] * 2
        dma, in_vmem, in_hbm = pltpu.SemaphoreType.DMA, pl.BlockSpec(memory_space=pltpu.VMEM), pl.BlockSpec(memory_space=pltpu.HBM)
        slots = [pltpu.HBM((n, *one), BF16) for n in (4, 3, 2) for one in blocks] + [pltpu.HBM(blocks[LENT], F32)] * 2
        out = pl.pallas_call(
            functools.partial(kernel, count),
            out_shape=[pltpu.VMEM(*one) for one in results] + slots,
            in_specs=[in_hbm] * 12,
            out_specs=[in_vmem] * 9 + [in_hbm] * 11,
            scratch_shapes=[pltpu.VMEM((2, *one), BF16) for one in chunk]
            + [pltpu.VMEM(chunk[0], F32)] * 2
            + [pltpu.VMEM((GROUP, 8, 128), F32), pltpu.VMEM((8, 128), F32)]
            + [dma((n,)) for n in (4, 4, 4, 24, 24, 36, 24, 4, 8, 8, 36, 48, 36, 24, 48, 4, 4, 4, 4, 6)],
            compiler_params=pltpu.CompilerParams(collective_id=0, has_side_effects=True, vmem_limit_bytes=LIMIT),
            name="step",
        )(*(pltpu.with_memory_space_constraint(one, pltpu.HBM) for one in arrays))[:9]
        return pl.pallas_call(
            finish,
            out_shape=[jax.ShapeDtypeStruct(*one) for one in results],
            in_specs=[in_vmem] * 9,
            out_specs=[pl.BlockSpec(memory_space=pl.ANY)] * 9,
            scratch_shapes=[dma((9, 2))],
            compiler_params=pltpu.CompilerParams(vmem_limit_bytes=LIMIT),
            name="finish",
        )(*(pltpu.with_memory_space_constraint(one, pltpu.VMEM) for one in out))

    all_of, cut = P(None, None, None), P(None, "dp", None)
    return jax.shard_map(
        step,
        mesh=mesh,
        in_specs=(P(("rep", "dp"), None, None, None),) * 3 + (all_of,) * 3 + (cut,) * 6,
        out_specs=(P("rep", None, None),) * 3 + (P("rep", "dp", None),) * 6,
        check_vma=False,
    )
```

time: 723 us -> 664 us (0.918)
  local copies, waits for them, and re-layouts: 26.3 us -> 0 us
  Pallas kernels: 678 us -> 662 us
  other arithmetic: 15.8 us -> 0 us
    unnamed x25 -> x0, local copies, waits for them, and re-layouts: 25.7 us -> none
    pallas_call x1 -> x2, Pallas kernels: 678 us -> 662 us  [the longest x1 642 us: step(): pl.pallas_call(functools.partial(kernel, count), out_shape=[pltpu.VMEM(*o...]
    add x2 -> x0, other arithmetic: 15.8 us -> none  [step(): new_v.append(0.95 * v1 + 0.05 * one * one)]
where the time goes in v2:
time: 664 us; the launch traced here: 662 us
  Pallas kernels  662 us (100%)
    pallas_call x1, Pallas kernels, step(): pl.pallas_call(functools.partial(kernel, count), out_shape=[pltpu.VMEM(*o...  642 us
    pallas_call x1, Pallas kernels, step(): pl.pallas_call(finish, out_shape=[jax.ShapeDtypeStruct(*one) for one in r...  19.5 us

profile of v2, /device:TPU:0, one launch (start us, length us, event | category | flops | bytes accessed | tf_op | source)
XLA Modules:
  0.0 662.4 jit_solution(11070306938323753722)
XLA Ops:
  0.6 642.2 %step.1 = (bf16[2,1024,3328]{2,1,0:T(8,128)(2,1)S(1)}, bf16[2,1024,3328]{2,1,0:T(8,128)(2,1)S(1)}, bf16[2,3328,1024]{2,1,0:T(8,128)(2,1)S(1)}, f32[2,128,3328]{2...) custom-call(bf16[1,2,1024,3328]{3,2,1,0:T(8,128)(2,1)} %refs_0_.1, ...), custom_call_target="tpu_custom_call" | custom-call | tf_op jit(solution)/shard_map/step/pallas_call | solution.py:454
  642.9 19.5 %finish.1 = (bf16[2,1024,3328]{2,1,0:T(8,128)(2,1)}, bf16[2,1024,3328]{2,1,0:T(8,128)(2,1)}, bf16[2,3328,1024]{2,1,0:T(8,128)(2,1)}, f32[2,128,3328]{2,1,0:T(8,1...) custom-call(bf16[2,1024,3328]{2,1,0:T(8,128)(2,1)S(1)} %get-tuple-el, ...), custom_call_target="tpu_custom_call" | custom-call | tf_op jit(solution)/shard_map/finish/pallas_call | solution.py:466

commit v3 on v2

--- a/solution.py
+++ b/solution.py
@@ -11,9 +11,8 @@
 HALVES = 2
 CHUNKS = 4
 GROUP = 8
-LENT = 0
-ORDER = (1, 2, 0)
-OUTR, OUTL = 4, 6
+OUTR, OUTL = 3, 5
+LAG = 2
 LIMIT = 5 * 2**20
 ROWS = 16
 
@@ -22,10 +21,8 @@
     g, w, m, v = refs[0:3], refs[3:6], refs[6:9], refs[9:12]
     t, nm, nv = refs[12:15], refs[15:18], refs[18:21]
     x, ein, iin = refs[21:24], refs[24:27], refs[27:30]
-    xm, xv = refs[30:32]
-    wb, lm, lv = refs[32:34], refs[34], refs[35]
-    nb, fbuf = refs[36:38]
-    (ld, osr, osl, xs, xr, er, ir, up, ns, nr, ar, pr, so, si, sp, ms, mr, hs, hr, mo) = refs[38:]
+    wb, nb, fbuf = refs[30:32], refs[32], refs[33]
+    (ld, osr, osl, xs, xr, er, ir, up, ns, nr, ar, pr, so, si, sp, gs, gr, mo) = refs[34:]
 
     me = lax.axis_index("dp")
     z, k = me // 2, me % 2
@@ -54,7 +51,7 @@
 
     def slot_start(c, i):
         rows, half = rows_of[c + 1], half_of[c + 1]
-        return pl.multiple_of(((2 * z + k) * rows + rows + i * half) % (GROUP * rows), 16)
+        return pl.multiple_of(((2 * z + k) * rows + 3 * rows + i * half) % (GROUP * rows), 16)
 
     def staged(c, i):
         return t[c + 1].at[0, pl.ds(slot_start(c, i), half_of[c + 1]), :]
@@ -79,6 +76,14 @@
             for l in range(2):
                 swap(J, a, l).start()
 
+    order = [(p, a) for p in range(2) for a in range(3)]
+
+    def give_next(n):
+        if n < len(order):
+            p, a = order[n]
+            give_terms(3 - p, (a,))
+            give_terms(p, (a,))
+
     give_terms(3, (0,))
 
     own_J = jnp.where(is_end, 0, 1)
@@ -86,7 +91,7 @@
     def old_weight(a, q, J=own_J):
         return pltpu.make_async_copy(full(w[a], a, J, k, q), wb[kind[a]].at[q % 2], up.at[q % 2])
 
-    old_weight(ORDER[0], 0).start()
+    old_weight(0, 0).start()
 
     def moments(a):
         return pltpu.make_async_copy(m[a], nm[a], mo.at[a]), pltpu.make_async_copy(v[a], nv[a], mo.at[3 + a])
@@ -131,13 +136,13 @@
         lax.fori_loop(0, half_of[a] // ROWS, row, 0)
         copy.start()
 
-    def final(a, J, q, more, acc):
+    def final(a, J, into, q, more, acc):
         l, s = at_layer(q)
         n = load(a, J, q, more)
 
         def row(r, acc):
             one = total(a, n, r)
-            t[a][l, pl.ds(pl.multiple_of((2 * z + k) * rows_of[a] + s * half_of[a] + r * ROWS, ROWS), ROWS), :] = one
+            t[a][l, pl.ds(pl.multiple_of((2 * chip(into) + k) * rows_of[a] + s * half_of[a] + r * ROWS, ROWS), ROWS), :] = one
             one = one.astype(F32)
             one = one * one
             for i in range(one.shape[1] // 128):
@@ -146,12 +151,16 @@
 
         return lax.fori_loop(0, half_of[a] // ROWS, row, acc)
 
-    def more_terms(p, a, q):
-        if p == 0 and a == 0:
+    def more_terms(n, q):
+        if n == 0:
 
             @pl.when(q == 1)
             def _():
-                give_terms(3, (1, 2))
+                give_terms(0, (0,))
+                give_next(1)
+
+    def sum_for_mid(a, q, to):
+        return remote(full(t[a], a, 3, k, q), full(t[a], a, 1, k, q), gs.at[a * CHUNKS + q], gr.at[a * CHUNKS + q], to)
 
     def from_end(a, p, q):
         i = p * 12 + a * CHUNKS + q
@@ -160,16 +169,6 @@
     def from_inner(a, p, q):
         i = p * 12 + a * CHUNKS + q
         return remote(part(iin[a].at[p], a, q), part(iin[a].at[p], a, q), osr.at[0], ir.at[i], inner)
-
-    def lend(l):
-        return (
-            remote(m[LENT].at[l], xm.at[l], ms.at[l], mr.at[l], outer),
-            remote(v[LENT].at[l], xv.at[l], ms.at[2 + l], mr.at[2 + l], outer),
-        )
-
-    def lend_sum(q):
-        here = full(t[LENT], LENT, 1, k, q)
-        return remote(here, here, hs.at[q], hr.at[q], outer)
 
     def loop(body):
         lax.fori_loop(0, CHUNKS, lambda q, _: (body(q), 0)[1], 0)
@@ -185,27 +184,36 @@
     @pl.when(is_end)
     def _():
         acc = zero
-        for p in range(3):
-            for a in range(3):
-
-                if p == 0 and a > 0:
-                    give_terms((0, 2)[a - 1])
-                if p == 1 and a == 0:
-                    give_terms(1)
-                if p == 1:
+        for n in range(len(order) + 1):
+            if n > 0:
+                give_next(n + 1)
+            if n == 3:
+                for a in range(3):
                     for copy in moments(a):
                         copy.start()
 
-                def both(q, acc, p=p, a=a):
+            def both(q, acc, n=n):
+                more_terms(n, q)
+                if n < len(order):
+                    p, a = order[n]
                     i = p * 12 + a * CHUNKS + q
-                    more_terms(p, a, q)
                     send(a, 3 - p, q, [], OUTR, osr, part(ein[a].at[p], a, q), er.at[i], inner, p == 0 and a != 1)
-                    if p == 1:
-                        from_inner(a, 0, q).wait_recv()
-                        acc = final(a, 0, q, [part(iin[a].at[0], a, q)], acc)
-                    return acc
-
-                acc = lax.fori_loop(0, CHUNKS, both, acc)
+                if n > 0:
+                    p, a = order[n - 1]
+                    from_inner(a, p, q).wait_recv()
+                    acc = final(a, p, (0, 3)[p], q, [part(iin[a].at[p], a, q)], acc)
+                if n == len(order):
+                    @pl.when(q > 0)
+                    def _():
+                        sum_for_mid(0, q - 1, inner).wait_send()
+
+                    @pl.when(q < CHUNKS - 1)
+                    def _():
+                        sum_for_mid(0, q, inner).start()
+
+                return acc
+
+            acc = lax.fori_loop(0, CHUNKS, both, acc)
         fbuf[...] = acc[:8] + acc[8:]
         drain(OUTR, osr)
 
@@ -216,44 +224,34 @@
             i = p * 12 + a * CHUNKS + q
             send(a, 3 - p, q, [part(ein[a].at[p], a, q)], OUTR, osr, part(iin[a].at[p], a, q), ir.at[i], inner, p == 0 and a != 1)
 
-        def outward(a, q):
-            from_inner(a, 0, q).wait_recv()
-            send(a, 0, q, [part(iin[a].at[0], a, q)], OUTL, osl, part(iin[a].at[0], a, q), ir.at[a * CHUNKS + q], outer, a != 1)
-
-        for copy in lend(0):
-            copy.start()
-        for a in range(4):
-            if a > 0:
-                give_terms((0, 2, 1)[a - 1])
-
-            def both(q, a=a):
-                more_terms(0, a, q)
-                if a < 3:
-                    inward(0, a, q)
-                if a > 0:
-                    outward(a - 1, q)
-
-            loop(both)
-        for copy in lend(1):
-            copy.start()
-        for a in range(3):
-            for copy in moments(a):
-                copy.start()
-        for a in range(3):
-            loop(functools.partial(inward, 1, a))
-        acc = zero
-        for a in range(3):
-
-            def last(q, acc, a=a):
-                from_inner(a, 1, q).wait_recv()
-                from_end(a, 2, q).wait_recv()
-                acc = final(a, 1, q, [part(ein[a].at[2], a, q), part(iin[a].at[1], a, q)], acc)
-                if a == LENT:
-                    lend_sum(q).start()
-                return acc
-
-            acc = lax.fori_loop(0, CHUNKS, last, acc)
-        fbuf[...] = acc[:8] + acc[8:]
+        def outward(p, a, q):
+            from_inner(a, p, q).wait_recv()
+            i = p * 12 + a * CHUNKS + q
+            send(a, p, q, [part(iin[a].at[p], a, q)], OUTL, osl, part(iin[a].at[p], a, q), ir.at[i], outer, p == 0 and a != 1)
+
+        for n in range(len(order) + 1):
+            if n > 0:
+                give_next(n + 1)
+            if n == 3:
+                for a in range(3):
+                    for copy in moments(a):
+                        copy.start()
+
+            def early(q, n=n):
+                more_terms(n, q)
+                if n < len(order):
+                    inward(*order[n], q)
+                if n > 0:
+                    outward(*order[n - 1], q + CHUNKS - LAG)
+
+            def late(q, n=n):
+                inward(*order[n], q)
+                outward(*order[n], q - LAG)
+
+            lax.fori_loop(0, LAG, lambda q, _: (early(q), 0)[1], 0)
+            if n < len(order):
+                lax.fori_loop(LAG, CHUNKS, lambda q, _: (late(q), 0)[1], 0)
+        fbuf[...] = zero[:8]
         drain(OUTR, osr)
         drain(OUTL, osl)
 
@@ -261,6 +259,13 @@
     sums = [remote(nb.at[me], nb.at[me], ns.at[d], nr.at[d], (me + d) % GROUP) for d in range(1, GROUP)]
     for copy in sums:
         copy.start()
+
+    @pl.when(is_end)
+    def _():
+        sum_for_mid(0, CHUNKS - 1, inner).start()
+        for a in (1, 2):
+            loop(lambda q, a=a: sum_for_mid(a, q, inner).start())
+
     for copy in sums:
         copy.wait()
 
@@ -280,90 +285,72 @@
         if to_outer is not None:
             remote(src, dst, so.at[to_outer * 12 + c], ar.at[to_outer * 12 + c], outer).start()
 
-    def stepped(a, q, J, mv, at_row):
+    def stepped(a, q):
         c, slot = kind[a], q % 2
         l, s = at_layer(q)
-        start = (2 * chip(J) + k) * rows_of[a] + s * half_of[a]
+        start = (2 * z + k) * rows_of[a] + s * half_of[a]
 
         def row(r, _):
             here = pl.ds(pl.multiple_of(r * ROWS, ROWS), ROWS)
             there = pl.ds(pl.multiple_of(start + r * ROWS, ROWS), ROWS)
-            those = pl.ds(pl.multiple_of(at_row + r * ROWS, ROWS), ROWS)
-            (m_in, v_in), layer = mv, l if len(mv[0].shape) == 3 else None
-            at = (those, slice(None)) if layer is None else (layer, those, slice(None))
+            those = pl.ds(pl.multiple_of(s * half_of[a] + r * ROWS, ROWS), ROWS)
             one = t[a][l, there, :].astype(F32) * fbuf[0:1, 0:1]
-            m1 = 0.9 * m_in[at] + 0.1 * one
-            v1 = 0.95 * v_in[at] + 0.05 * one * one
-            if layer is not None:
-                m_in[at] = m1
-                v_in[at] = v1
+            m1 = 0.9 * nm[a][l, those, :] + 0.1 * one
+            v1 = 0.95 * nv[a][l, those, :] + 0.05 * one * one
+            nm[a][l, those, :] = m1
+            nv[a][l, those, :] = v1
             old = wb[c][slot, here, :].astype(F32)
             t[a][l, there, :] = (old - 0.02 * (m1 * lax.rsqrt(v1 + 1e-8) + 0.1 * old)).astype(BF16)
             return 0
 
         lax.fori_loop(0, half_of[a] // ROWS, row, 0)
 
-    for n, a in enumerate(ORDER):
-        if a == LENT:
-
-            @pl.when(jnp.logical_not(is_end))
-            def _():
-                for q in range(CHUNKS):
-                    lend_sum(q).wait_send()
-
+    for a in range(3):
         for copy in moments(a):
             copy.wait()
 
-        def update(q, n=n, a=a):
+        def update(q, a=a):
             old_weight(a, q).wait()
 
             @pl.when(q < CHUNKS - 1)
             def _():
                 old_weight(a, q + 1).start()
 
-            if n < 2:
+            if a < 2:
 
                 @pl.when(q == CHUNKS - 1)
                 def _():
-                    old_weight(ORDER[n + 1], q * 0).start()
-
-            stepped(a, q, own_J, (nm[a], nv[a]), at_layer(q)[1] * half_of[a])
+                    old_weight(a + 1, q * 0).start()
+
+            @pl.when(jnp.logical_not(is_end))
+            def _():
+                sum_for_mid(a, q, outer).wait_recv()
+
+            stepped(a, q)
             src = full(t[a], a, own_J, k, q)
 
             @pl.when(is_end)
             def _():
-                give(a, q, 0, src, (0, 2), None)
+                give(a, q, 0, src, None, None)
 
             @pl.when(jnp.logical_not(is_end))
             def _():
-                give(a, q, 1, src, (0, 0), None if a == LENT else 0)
+                give(a, q, 1, src, (0, 0), 0)
 
         loop(update)
 
     @pl.when(is_end)
     def _():
-        def lent(q):
-            a = LENT
-            lend_sum(q).wait_recv()
-
-            @pl.when(q % HALVES == 0)
-            def _():
-                for copy in lend(q // HALVES):
-                    copy.wait_recv()
-
-            copies = (
-                pltpu.make_async_copy(part(xm, a, q), lm, up.at[2]),
-                pltpu.make_async_copy(part(xv, a, q), lv, up.at[3]),
-                old_weight(a, q, 1),
-            )
-            for copy in copies:
-                copy.start()
-            for copy in copies:
-                copy.wait()
-            stepped(a, q, 1, (lm, lv), 0)
-            give(a, q, 1, full(t[a], a, 1, k, q), None, None)
-
-        loop(lent)
+        sum_for_mid(0, CHUNKS - 1, inner).wait_send()
+        for a in (1, 2):
+            loop(lambda q, a=a: sum_for_mid(a, q, inner).wait_send())
+        for a in range(3):
+
+            def pass_on(q, a=a):
+                c, src = a * CHUNKS + q, full(t[a], a, 0, k, q)
+                remote(src, src, si.at[c], ar.at[24 + c], inner).start()
+
+            loop(pass_on)
 
     def arrived(a, q, J, slot):
         here = full(t[a], a, J, k, q)
@@ -372,9 +359,7 @@
     @pl.when(is_end)
     def _():
         for slot in range(3):
-            for a in ORDER:
-                if slot == 0 and a == LENT:
-                    continue
+            for a in range(3):
 
                 def on(q, a=a, slot=slot):
                     arrived(a, q, slot + 1, slot)
@@ -384,7 +369,7 @@
 
     @pl.when(jnp.logical_not(is_end))
     def _():
-        for a in ORDER:
+        for a in range(3):
 
             def on(q, a=a):
                 arrived(a, q, 2, 0)
@@ -393,7 +378,7 @@
                 give(a, q, 0, full(t[a], a, 0, k, q), (1, 1), None)
 
             loop(on)
-        for a in ORDER:
+        for a in range(3):
 
             def on(q, a=a):
                 arrived(a, q, 3, 1)
@@ -415,19 +400,13 @@
             @pl.when(jnp.logical_not(is_end))
             def _():
                 remote(here, here, si.at[12 + c], ar.at[c], inner).wait_send()
-                for n in range(1 if a == LENT else 0, 3):
+                for n in range(3):
                     remote(here, here, so.at[n * 12 + c], ar.at[c], outer).wait_send()
 
         loop(rest)
         for J in range(4):
             for l in range(2):
                 swap(J, a, l).wait_send()
-
-    @pl.when(jnp.logical_not(is_end))
-    def _():
-        for l in range(2):
-            for copy in lend(l):
-                copy.wait_send()
 
 
 def finish(*refs):
@@ -450,16 +429,15 @@
         chunk = [(one[1] // HALVES, one[2]) for one in pair]
         results = [(one.shape, BF16) for one in weights] + [(one, F32) for one in blocks] * 2
         dma, in_vmem, in_hbm = pltpu.SemaphoreType.DMA, pl.BlockSpec(memory_space=pltpu.VMEM), pl.BlockSpec(memory_space=pltpu.HBM)
-        slots = [pltpu.HBM((n, *one), BF16) for n in (4, 3, 2) for one in blocks] + [pltpu.HBM(blocks[LENT], F32)] * 2
+        slots = [pltpu.HBM((n, *one), BF16) for n in (4, 2, 2) for one in blocks]
         out = pl.pallas_call(
             functools.partial(kernel, count),
             out_shape=[pltpu.VMEM(*one) for one in results] + slots,
             in_specs=[in_hbm] * 12,
-            out_specs=[in_vmem] * 9 + [in_hbm] * 11,
+            out_specs=[in_vmem] * 9 + [in_hbm] * 9,
             scratch_shapes=[pltpu.VMEM((2, *one), BF16) for one in chunk]
-            + [pltpu.VMEM(chunk[0], F32)] * 2
             + [pltpu.VMEM((GROUP, 8, 128), F32), pltpu.VMEM((8, 128), F32)]
-            + [dma((n,)) for n in (4, 4, 4, 24, 24, 36, 24, 4, 8, 8, 36, 48, 36, 24, 48, 4, 4, 4, 4, 6)],
+            + [dma((n,)) for n in (4, 4, 4, 24, 24, 24, 24, 2, 8, 8, 36, 48, 36, 24, 48, 12, 12, 6)],
             compiler_params=pltpu.CompilerParams(collective_id=0, has_side_effects=True, vmem_limit_bytes=LIMIT),
             name="step",
         )(*(pltpu.with_memory_space_constraint(one, pltpu.HBM) for one in arrays))[:9]

time: 664 us -> 636 us (0.958)
  Pallas kernels: 662 us -> 634 us
    pallas_call x1, Pallas kernels: 642 us -> 614 us  [step(): pl.pallas_call(functools.partial(kernel, count), out_shape=[pltpu.VMEM(*o...]
where the time goes in v3:
time: 636 us; the launch traced here: 634 us
  Pallas kernels  634 us (100%)
    pallas_call x1, Pallas kernels, step(): pl.pallas_call(functools.partial(kernel, count), out_shape=[pltpu.VMEM(*o...  614 us
    pallas_call x1, Pallas kernels, step(): pl.pallas_call(finish, out_shape=[jax.ShapeDtypeStruct(*one) for one in r...  19.5 us

profile of v3, /device:TPU:0, one launch (start us, length us, event | category | flops | bytes accessed | tf_op | source)
XLA Modules:
  0.0 634.2 jit_solution(8352220079291207412)
XLA Ops:
  0.6 614.1 %step.1 = (bf16[2,1024,3328]{2,1,0:T(8,128)(2,1)S(1)}, bf16[2,1024,3328]{2,1,0:T(8,128)(2,1)S(1)}, bf16[2,3328,1024]{2,1,0:T(8,128)(2,1)S(1)}, f32[2,128,3328]{2...) custom-call(bf16[1,2,1024,3328]{3,2,1,0:T(8,128)(2,1)} %refs_0_.1, ...), custom_call_target="tpu_custom_call" | custom-call | tf_op jit(solution)/shard_map/step/pallas_call | solution.py:433
  614.7 19.5 %finish.1 = (bf16[2,1024,3328]{2,1,0:T(8,128)(2,1)}, bf16[2,1024,3328]{2,1,0:T(8,128)(2,1)}, bf16[2,3328,1024]{2,1,0:T(8,128)(2,1)}, f32[2,128,3328]{2,1,0:T(8,1...) custom-call(bf16[2,1024,3328]{2,1,0:T(8,128)(2,1)S(1)} %get-tuple-el, ...), custom_call_target="tpu_custom_call" | custom-call | tf_op jit(solution)/shard_map/finish/pallas_call | solution.py:444

commit v4 on v3

--- a/solution.py
+++ b/solution.py
@@ -8,11 +8,15 @@
 from jax.sharding import PartitionSpec as P
 
 F32, BF16 = jnp.float32, jnp.bfloat16
-HALVES = 2
-CHUNKS = 4
+CUTS = (4, 4, 2)
+CHUNKS = (8, 8, 4)
+BASE = (0, 8, 16)
+ALL = 20
+TURNS = 4
+ORDER = (0, 2, 1)
 GROUP = 8
 OUTR, OUTL = 3, 5
-LAG = 2
+LAG = 1
 LIMIT = 5 * 2**20
 ROWS = 16
 
@@ -32,21 +36,22 @@
     partner = 2 * z + 1 - k
     kind = (0, 0, 1)
     rows_of = [r.shape[1] for r in m]
-    half_of = [r // HALVES for r in rows_of]
+    half_of = [r // cuts for r, cuts in zip(rows_of, CUTS, strict=True)]
+    per = [n // TURNS for n in CHUNKS]
 
     def chip(J):
         return J + h * (3 - 2 * J)
 
-    def at_layer(q):
-        return q // HALVES, q % HALVES
+    def at_layer(a, q):
+        return q // CUTS[a], q % CUTS[a]
 
     def full(ref, a, J, parity, q):
-        l, s = at_layer(q)
+        l, s = at_layer(a, q)
         start = pl.multiple_of((2 * chip(J) + parity) * rows_of[a] + s * half_of[a], 16)
         return ref.at[l, pl.ds(start, half_of[a]), :]
 
     def part(ref, a, q):
-        l, s = at_layer(q)
+        l, s = at_layer(a, q)
         return ref.at[l, pl.ds(pl.multiple_of(s * half_of[a], 16), half_of[a]), :]
 
     def slot_start(c, i):
@@ -76,7 +81,7 @@
             for l in range(2):
                 swap(J, a, l).start()
 
-    order = [(p, a) for p in range(2) for a in range(3)]
+    order = [(p, a) for p in range(2) for a in ORDER]
 
     def give_next(n):
         if n < len(order):
@@ -84,20 +89,20 @@
             give_terms(3 - p, (a,))
             give_terms(p, (a,))
 
-    give_terms(3, (0,))
+    give_terms(3, ORDER[:1])
 
     own_J = jnp.where(is_end, 0, 1)
 
     def old_weight(a, q, J=own_J):
         return pltpu.make_async_copy(full(w[a], a, J, k, q), wb[kind[a]].at[q % 2], up.at[q % 2])
 
-    old_weight(0, 0).start()
+    old_weight(ORDER[0], 0).start()
 
     def moments(a):
         return pltpu.make_async_copy(m[a], nm[a], mo.at[a]), pltpu.make_async_copy(v[a], nv[a], mo.at[3 + a])
 
     def load(a, J, q, more):
-        l, s = at_layer(q)
+        l, s = at_layer(a, q)
 
         @pl.when(s == 0)
         def _():
@@ -137,7 +142,7 @@
         copy.start()
 
     def final(a, J, into, q, more, acc):
-        l, s = at_layer(q)
+        l, s = at_layer(a, q)
         n = load(a, J, q, more)
 
         def row(r, acc):
@@ -156,22 +161,25 @@
 
             @pl.when(q == 1)
             def _():
-                give_terms(0, (0,))
+                give_terms(0, ORDER[:1])
                 give_next(1)
 
     def sum_for_mid(a, q, to):
-        return remote(full(t[a], a, 3, k, q), full(t[a], a, 1, k, q), gs.at[a * CHUNKS + q], gr.at[a * CHUNKS + q], to)
+        return remote(full(t[a], a, 3, k, q), full(t[a], a, 1, k, q), gs.at[BASE[a] + q], gr.at[BASE[a] + q], to)
 
     def from_end(a, p, q):
-        i = p * 12 + a * CHUNKS + q
+        i = p * ALL + BASE[a] + q
         return remote(part(ein[a].at[p], a, q), part(ein[a].at[p], a, q), osr.at[0], er.at[i], outer)
 
     def from_inner(a, p, q):
-        i = p * 12 + a * CHUNKS + q
+        i = p * ALL + BASE[a] + q
         return remote(part(iin[a].at[p], a, q), part(iin[a].at[p], a, q), osr.at[0], ir.at[i], inner)
 
-    def loop(body):
-        lax.fori_loop(0, CHUNKS, lambda q, _: (body(q), 0)[1], 0)
+    def loop(a, body):
+        lax.fori_loop(0, CHUNKS[a], lambda q, _: (body(q), 0)[1], 0)
+
+    def turn(a, q):
+        return [(a, q * per[a] + i) for i in range(per[a])]
 
     zero = jnp.zeros((ROWS, 128), F32)
 
@@ -196,24 +204,28 @@
                 more_terms(n, q)
                 if n < len(order):
                     p, a = order[n]
-                    i = p * 12 + a * CHUNKS + q
-                    send(a, 3 - p, q, [], OUTR, osr, part(ein[a].at[p], a, q), er.at[i], inner, p == 0 and a != 1)
+                    for a, c in turn(a, q):
+                        i = p * ALL + BASE[a] + c
+                        send(a, 3 - p, c, [], OUTR, osr, part(ein[a].at[p], a, c), er.at[i], inner, p == 0 and a != 1)
                 if n > 0:
                     p, a = order[n - 1]
-                    from_inner(a, p, q).wait_recv()
-                    acc = final(a, p, (0, 3)[p], q, [part(iin[a].at[p], a, q)], acc)
+                    for a, c in turn(a, q):
+                        from_inner(a, p, c).wait_recv()
+                        acc = final(a, p, (0, 3)[p], c, [part(iin[a].at[p], a, c)], acc)
                 if n == len(order):
                     @pl.when(q > 0)
                     def _():
-                        sum_for_mid(0, q - 1, inner).wait_send()
-
-                    @pl.when(q < CHUNKS - 1)
+                        for a, c in turn(ORDER[0], q - 1):
+                            sum_for_mid(a, c, inner).wait_send()
+
+                    @pl.when(q < TURNS - 1)
                     def _():
-                        sum_for_mid(0, q, inner).start()
+                        for a, c in turn(ORDER[0], q):
+                            sum_for_mid(a, c, inner).start()
 
                 return acc
 
-            acc = lax.fori_loop(0, CHUNKS, both, acc)
+            acc = lax.fori_loop(0, TURNS, both, acc)
         fbuf[...] = acc[:8] + acc[8:]
         drain(OUTR, osr)
 
@@ -221,12 +233,12 @@
     def _():
         def inward(p, a, q):
             from_end(a, p, q).wait_recv()
-            i = p * 12 + a * CHUNKS + q
+            i = p * ALL + BASE[a] + q
             send(a, 3 - p, q, [part(ein[a].at[p], a, q)], OUTR, osr, part(iin[a].at[p], a, q), ir.at[i], inner, p == 0 and a != 1)
 
         def outward(p, a, q):
             from_inner(a, p, q).wait_recv()
-            i = p * 12 + a * CHUNKS + q
+            i = p * ALL + BASE[a] + q
             send(a, p, q, [part(iin[a].at[p], a, q)], OUTL, osl, part(iin[a].at[p], a, q), ir.at[i], outer, p == 0 and a != 1)
 
         for n in range(len(order) + 1):
@@ -237,20 +249,29 @@
                     for copy in moments(a):
                         copy.start()
 
+            def some(ins, outs):
+                for i in range(max(len(ins), len(outs))):
+                    if i < len(ins):
+                        inward(*ins[i])
+                    if i < len(outs):
+                        outward(*outs[i])
+
+            def chunks(n, q):
+                if not 0 <= n < len(order):
+                    return []
+                return [(order[n][0], a, c) for a, c in turn(order[n][1], q)]
+
             def early(q, n=n):
                 more_terms(n, q)
-                if n < len(order):
-                    inward(*order[n], q)
-                if n > 0:
-                    outward(*order[n - 1], q + CHUNKS - LAG)
+                some(chunks(n, q), chunks(n - 1, q + TURNS - LAG))
 
             def late(q, n=n):
-                inward(*order[n], q)
-                outward(*order[n], q - LAG)
+                more_terms(n, q)
+                some(chunks(n, q), chunks(n, q - LAG))
 
             lax.fori_loop(0, LAG, lambda q, _: (early(q), 0)[1], 0)
             if n < len(order):
-                lax.fori_loop(LAG, CHUNKS, lambda q, _: (late(q), 0)[1], 0)
+                lax.fori_loop(LAG, TURNS, lambda q, _: (late(q), 0)[1], 0)
         fbuf[...] = zero[:8]
         drain(OUTR, osr)
         drain(OUTL, osl)
@@ -262,9 +283,10 @@
 
     @pl.when(is_end)
     def _():
-        sum_for_mid(0, CHUNKS - 1, inner).start()
-        for a in (1, 2):
-            loop(lambda q, a=a: sum_for_mid(a, q, inner).start())
+        for a, q in turn(ORDER[0], TURNS - 1):
+            sum_for_mid(a, q, inner).start()
+        for a in ORDER[1:]:
+            loop(a, lambda q, a=a: sum_for_mid(a, q, inner).start())
 
     for copy in sums:
         copy.wait()
@@ -277,17 +299,17 @@
     fbuf[...] = jnp.broadcast_to(factor, fbuf.shape)
 
     def give(a, q, J, src, to_inner, to_outer):
-        c = a * CHUNKS + q
+        c = BASE[a] + q
         dst = full(t[a], a, J, k, q)
-        remote(src, dst, sp.at[J * 12 + c], pr.at[J * 12 + c], partner).start()
+        remote(src, dst, sp.at[J * ALL + c], pr.at[J * ALL + c], partner).start()
         if to_inner is not None:
-            remote(src, dst, si.at[to_inner[0] * 12 + c], ar.at[to_inner[1] * 12 + c], inner).start()
+            remote(src, dst, si.at[to_inner[0] * ALL + c], ar.at[to_inner[1] * ALL + c], inner).start()
         if to_outer is not None:
-            remote(src, dst, so.at[to_outer * 12 + c], ar.at[to_outer * 12 + c], outer).start()
+            remote(src, dst, so.at[to_outer * ALL + c], ar.at[to_outer * ALL + c], outer).start()
 
     def stepped(a, q):
         c, slot = kind[a], q % 2
-        l, s = at_layer(q)
+        l, s = at_layer(a, q)
         start = (2 * z + k) * rows_of[a] + s * half_of[a]
 
         def row(r, _):
@@ -305,22 +327,22 @@
 
         lax.fori_loop(0, half_of[a] // ROWS, row, 0)
 
-    for a in range(3):
+    for n, a in enumerate(ORDER):
         for copy in moments(a):
             copy.wait()
 
-        def update(q, a=a):
+        def update(q, n=n, a=a):
             old_weight(a, q).wait()
 
-            @pl.when(q < CHUNKS - 1)
+            @pl.when(q < CHUNKS[a] - 1)
             def _():
                 old_weight(a, q + 1).start()
 
-            if a < 2:
-
-                @pl.when(q == CHUNKS - 1)
+            if n < 2:
+
+                @pl.when(q == CHUNKS[a] - 1)
                 def _():
-                    old_weight(a + 1, q * 0).start()
+                    old_weight(ORDER[n + 1], q * 0).start()
 
             @pl.when(jnp.logical_not(is_end))
             def _():
@@ -337,39 +359,40 @@
             def _():
                 give(a, q, 1, src, (0, 0), 0)
 
-        loop(update)
+        loop(a, update)
 
     @pl.when(is_end)
     def _():
-        sum_for_mid(0, CHUNKS - 1, inner).wait_send()
-        for a in (1, 2):
-            loop(lambda q, a=a: sum_for_mid(a, q, inner).wait_send())
-        for a in range(3):
+        for a, q in turn(ORDER[0], TURNS - 1):
+            sum_for_mid(a, q, inner).wait_send()
+        for a in ORDER[1:]:
+            loop(a, lambda q, a=a: sum_for_mid(a, q, inner).wait_send())
+        for a in ORDER:
 
             def pass_on(q, a=a):
-                c, src = a * CHUNKS + q, full(t[a], a, 0, k, q)
-                remote(src, src, si.at[c], ar.at[24 + c], inner).start()
-
-            loop(pass_on)
+                c, src = BASE[a] + q, full(t[a], a, 0, k, q)
+                remote(src, src, si.at[c], ar.at[2 * ALL + c], inner).start()
+
+            loop(a, pass_on)
 
     def arrived(a, q, J, slot):
         here = full(t[a], a, J, k, q)
-        remote(here, here, sp.at[0], ar.at[slot * 12 + a * CHUNKS + q], inner).wait_recv()
+        remote(here, here, sp.at[0], ar.at[slot * ALL + BASE[a] + q], inner).wait_recv()
 
     @pl.when(is_end)
     def _():
         for slot in range(3):
-            for a in range(3):
+            for a in ORDER:
 
                 def on(q, a=a, slot=slot):
                     arrived(a, q, slot + 1, slot)
                     give(a, q, slot + 1, full(t[a], a, slot + 1, k, q), None, None)
 
-                loop(on)
+                loop(a, on)
 
     @pl.when(jnp.logical_not(is_end))
     def _():
-        for a in range(3):
+        for a in ORDER:
 
             def on(q, a=a):
                 arrived(a, q, 2, 0)
@@ -377,33 +400,33 @@
                 arrived(a, q, 0, 2)
                 give(a, q, 0, full(t[a], a, 0, k, q), (1, 1), None)
 
-            loop(on)
-        for a in range(3):
+            loop(a, on)
+        for a in ORDER:
 
             def on(q, a=a):
                 arrived(a, q, 3, 1)
                 give(a, q, 3, full(t[a], a, 3, k, q), None, 2)
 
-            loop(on)
+            loop(a, on)
 
     for a in range(3):
 
         def rest(q, a=a):
-            c = a * CHUNKS + q
+            c = BASE[a] + q
             for J in range(4):
                 mine, theirs = full(t[a], a, J, k, q), full(t[a], a, J, 1 - k, q)
-                remote(mine, mine, sp.at[J * 12 + c], pr.at[J * 12 + c], partner).wait_send()
-                remote(theirs, theirs, sp.at[J * 12 + c], pr.at[J * 12 + c], partner).wait_recv()
+                remote(mine, mine, sp.at[J * ALL + c], pr.at[J * ALL + c], partner).wait_send()
+                remote(theirs, theirs, sp.at[J * ALL + c], pr.at[J * ALL + c], partner).wait_recv()
             here = full(t[a], a, own_J, k, q)
             remote(here, here, si.at[c], ar.at[c], inner).wait_send()
 
             @pl.when(jnp.logical_not(is_end))
             def _():
-                remote(here, here, si.at[12 + c], ar.at[c], inner).wait_send()
+                remote(here, here, si.at[ALL + c], ar.at[c], inner).wait_send()
                 for n in range(3):
-                    remote(here, here, so.at[n * 12 + c], ar.at[c], outer).wait_send()
-
-        loop(rest)
+                    remote(here, here, so.at[n * ALL + c], ar.at[c], outer).wait_send()
+
+        loop(a, rest)
         for J in range(4):
             for l in range(2):
                 swap(J, a, l).wait_send()
@@ -426,7 +449,7 @@
         blocks = [one.shape for one in m]
         count = GROUP * sum(one.size for one in m)
         pair = (blocks[0], blocks[2])
-        chunk = [(one[1] // HALVES, one[2]) for one in pair]
+        chunk = [(one[1] // cuts, one[2]) for one, cuts in zip(pair, CUTS[1:], strict=True)]
         results = [(one.shape, BF16) for one in weights] + [(one, F32) for one in blocks] * 2
         dma, in_vmem, in_hbm = pltpu.SemaphoreType.DMA, pl.BlockSpec(memory_space=pltpu.VMEM), pl.BlockSpec(memory_space=pltpu.HBM)
         slots = [pltpu.HBM((n, *one), BF16) for n in (4, 2, 2) for one in blocks]
@@ -437,7 +460,7 @@
             out_specs=[in_vmem] * 9 + [in_hbm] * 9,
             scratch_shapes=[pltpu.VMEM((2, *one), BF16) for one in chunk]
             + [pltpu.VMEM((GROUP, 8, 128), F32), pltpu.VMEM((8, 128), F32)]
-            + [dma((n,)) for n in (4, 4, 4, 24, 24, 24, 24, 2, 8, 8, 36, 48, 36, 24, 48, 12, 12, 6)],
+            + [dma((n,)) for n in (4, 4, 4, 24, 24, 2 * ALL, 2 * ALL, 2, 8, 8, 3 * ALL, 4 * ALL, 3 * ALL, 2 * ALL, 4 * ALL, ALL, ALL, 6)],
             compiler_params=pltpu.CompilerParams(collective_id=0, has_side_effects=True, vmem_limit_bytes=LIMIT),
             name="step",
         )(*(pltpu.with_memory_space_constraint(one, pltpu.HBM) for one in arrays))[:9]

time: 636 us -> 622 us (0.978)
  Pallas kernels: 634 us -> 619 us
    pallas_call x1, Pallas kernels: 614 us -> 599 us  [step(): pl.pallas_call(functools.partial(kernel, count), out_shape=[pltpu.VMEM(*o...]
where the time goes in v4:
time: 622 us; the launch traced here: 619 us
  Pallas kernels  619 us (100%)
    pallas_call x1, Pallas kernels, step(): pl.pallas_call(functools.partial(kernel, count), out_shape=[pltpu.VMEM(*o...  599 us
    pallas_call x1, Pallas kernels, step(): pl.pallas_call(finish, out_shape=[jax.ShapeDtypeStruct(*one) for one in r...  19.5 us

profile of v4, /device:TPU:0, one launch (start us, length us, event | category | flops | bytes accessed | tf_op | source)
XLA Modules:
  0.0 619.2 jit_solution(15394333707924393875)
XLA Ops:
  0.6 599.1 %step.1 = (bf16[2,1024,3328]{2,1,0:T(8,128)(2,1)S(1)}, bf16[2,1024,3328]{2,1,0:T(8,128)(2,1)S(1)}, bf16[2,3328,1024]{2,1,0:T(8,128)(2,1)S(1)}, f32[2,128,3328]{2...) custom-call(bf16[1,2,1024,3328]{3,2,1,0:T(8,128)(2,1)} %refs_0_.1, ...), custom_call_target="tpu_custom_call" | custom-call | tf_op jit(solution)/shard_map/step/pallas_call | solution.py:456
  599.7 19.5 %finish.1 = (bf16[2,1024,3328]{2,1,0:T(8,128)(2,1)}, bf16[2,1024,3328]{2,1,0:T(8,128)(2,1)}, bf16[2,3328,1024]{2,1,0:T(8,128)(2,1)}, f32[2,128,3328]{2,1,0:T(8,1...) custom-call(bf16[2,1024,3328]{2,1,0:T(8,128)(2,1)S(1)} %get-tuple-el, ...), custom_call_target="tpu_custom_call" | custom-call | tf_op jit(solution)/shard_map/finish/pallas_call | solution.py:467

commit v5 on v4

--- a/solution.py
+++ b/solution.py
@@ -14,8 +14,9 @@
 ALL = 20
 TURNS = 4
 ORDER = (0, 2, 1)
+KEPT = 2
 GROUP = 8
-OUTR, OUTL = 3, 5
+OUTR, OUTL = 4, 6
 LAG = 1
 LIMIT = 5 * 2**20
 ROWS = 16
@@ -101,10 +102,10 @@
     def moments(a):
         return pltpu.make_async_copy(m[a], nm[a], mo.at[a]), pltpu.make_async_copy(v[a], nv[a], mo.at[3 + a])
 
-    def load(a, J, q, more):
+    def load(a, J, q, more, first_layer=False):
         l, s = at_layer(a, q)
 
-        @pl.when(s == 0)
+        @pl.when(q == 0 if first_layer else s == 0)
         def _():
             remote(x[a].at[J, l], x[a].at[J, l], xs.at[J * 6 + a * 2 + l], xr.at[J * 6 + a * 2 + l], partner).wait_recv()
 
@@ -141,9 +142,9 @@
         lax.fori_loop(0, half_of[a] // ROWS, row, 0)
         copy.start()
 
-    def final(a, J, into, q, more, acc):
+    def final(a, J, into, q, more, acc, first_layer=False):
         l, s = at_layer(a, q)
-        n = load(a, J, q, more)
+        n = load(a, J, q, more, first_layer)
 
         def row(r, acc):
             one = total(a, n, r)
@@ -175,6 +176,9 @@
         i = p * ALL + BASE[a] + q
         return remote(part(iin[a].at[p], a, q), part(iin[a].at[p], a, q), osr.at[0], ir.at[i], inner)
 
+    def given(a):
+        return CHUNKS[a] - KEPT if a == ORDER[-1] else CHUNKS[a]
+
     def loop(a, body):
         lax.fori_loop(0, CHUNKS[a], lambda q, _: (body(q), 0)[1], 0)
 
@@ -199,6 +203,13 @@
                 for a in range(3):
                     for copy in moments(a):
                         copy.start()
+
+            if n == len(order):
+                a = ORDER[-1]
+                l = CHUNKS[a] // CUTS[a] - 1
+                swap(1, a, l).wait_recv()
+                for c in range(CHUNKS[a] - KEPT, CHUNKS[a]):
+                    send(a, 1, c, [], OUTR, osr, part(ein[a].at[2], a, c), er.at[2 * ALL + BASE[a] + c], inner, False)
 
             def both(q, acc, n=n):
                 more_terms(n, q)
@@ -211,21 +222,10 @@
                     p, a = order[n - 1]
                     for a, c in turn(a, q):
                         from_inner(a, p, c).wait_recv()
-                        acc = final(a, p, (0, 3)[p], c, [part(iin[a].at[p], a, c)], acc)
-                if n == len(order):
-                    @pl.when(q > 0)
-                    def _():
-                        for a, c in turn(ORDER[0], q - 1):
-                            sum_for_mid(a, c, inner).wait_send()
-
-                    @pl.when(q < TURNS - 1)
-                    def _():
-                        for a, c in turn(ORDER[0], q):
-                            sum_for_mid(a, c, inner).start()
-
+                        acc = final(a, p, (0, 3)[p], c, [part(iin[a].at[p], a, c)], acc, n == len(order))
                 return acc
 
-            acc = lax.fori_loop(0, TURNS, both, acc)
+            acc = lax.fori_loop(0, TURNS if n < len(order) else TURNS - 1, both, acc)
         fbuf[...] = acc[:8] + acc[8:]
         drain(OUTR, osr)
 
@@ -269,10 +269,15 @@
                 more_terms(n, q)
                 some(chunks(n, q), chunks(n, q - LAG))
 
-            lax.fori_loop(0, LAG, lambda q, _: (early(q), 0)[1], 0)
             if n < len(order):
+                lax.fori_loop(0, LAG, lambda q, _: (early(q), 0)[1], 0)
                 lax.fori_loop(LAG, TURNS, lambda q, _: (late(q), 0)[1], 0)
-        fbuf[...] = zero[:8]
+        acc, a = zero, ORDER[-1]
+        for c in range(CHUNKS[a] - KEPT, CHUNKS[a]):
+            from_inner(a, 1, c).wait_recv()
+            from_end(a, 2, c).wait_recv()
+            acc = final(a, 1, 1, c, [part(iin[a].at[1], a, c), part(ein[a].at[2], a, c)], acc)
+        fbuf[...] = acc[:8] + acc[8:]
         drain(OUTR, osr)
         drain(OUTL, osl)
 
@@ -281,12 +286,11 @@
     for copy in sums:
         copy.start()
 
+
     @pl.when(is_end)
     def _():
-        for a, q in turn(ORDER[0], TURNS - 1):
-            sum_for_mid(a, q, inner).start()
-        for a in ORDER[1:]:
-            loop(a, lambda q, a=a: sum_for_mid(a, q, inner).start())
+        for a in ORDER:
+            lax.fori_loop(0, given(a), lambda q, _, a=a: (sum_for_mid(a, q, inner).start(), 0)[1], 0)
 
     for copy in sums:
         copy.wait()
@@ -344,7 +348,7 @@
                 def _():
                     old_weight(ORDER[n + 1], q * 0).start()
 
-            @pl.when(jnp.logical_not(is_end))
+            @pl.when(jnp.logical_and(jnp.logical_not(is_end), q < given(a)))
             def _():
                 sum_for_mid(a, q, outer).wait_recv()
 
@@ -363,10 +367,8 @@
 
     @pl.when(is_end)
     def _():
-        for a, q in turn(ORDER[0], TURNS - 1):
-            sum_for_mid(a, q, inner).wait_send()
-        for a in ORDER[1:]:
-            loop(a, lambda q, a=a: sum_for_mid(a, q, inner).wait_send())
+        for a in ORDER:
+            lax.fori_loop(0, given(a), lambda q, _, a=a: (sum_for_mid(a, q, inner).wait_send(), 0)[1], 0)
         for a in ORDER:
 
             def pass_on(q, a=a):
@@ -452,7 +454,7 @@
         chunk = [(one[1] // cuts, one[2]) for one, cuts in zip(pair, CUTS[1:], strict=True)]
         results = [(one.shape, BF16) for one in weights] + [(one, F32) for one in blocks] * 2
         dma, in_vmem, in_hbm = pltpu.SemaphoreType.DMA, pl.BlockSpec(memory_space=pltpu.VMEM), pl.BlockSpec(memory_space=pltpu.HBM)
-        slots = [pltpu.HBM((n, *one), BF16) for n in (4, 2, 2) for one in blocks]
+        slots = [pltpu.HBM((n, *one), BF16) for n in (4, 3, 2) for one in blocks]
         out = pl.pallas_call(
             functools.partial(kernel, count),
             out_shape=[pltpu.VMEM(*one) for one in results] + slots,
@@ -460,7 +462,7 @@
             out_specs=[in_vmem] * 9 + [in_hbm] * 9,
             scratch_shapes=[pltpu.VMEM((2, *one), BF16) for one in chunk]
             + [pltpu.VMEM((GROUP, 8, 128), F32), pltpu.VMEM((8, 128), F32)]
-            + [dma((n,)) for n in (4, 4, 4, 24, 24, 2 * ALL, 2 * ALL, 2, 8, 8, 3 * ALL, 4 * ALL, 3 * ALL, 2 * ALL, 4 * ALL, ALL, ALL, 6)],
+            + [dma((n,)) for n in (4, 4, 4, 24, 24, 3 * ALL, 2 * ALL, 2, 8, 8, 3 * ALL, 4 * ALL, 3 * ALL, 2 * ALL, 4 * ALL, ALL, ALL, 6)],
             compiler_params=pltpu.CompilerParams(collective_id=0, has_side_effects=True, vmem_limit_bytes=LIMIT),
             name="step",
         )(*(pltpu.with_memory_space_constraint(one, pltpu.HBM) for one in arrays))[:9]

time: 622 us -> 616 us (level)
  no operation moved by 1% of the time
where the time goes in v5:
time: 616 us; the launch traced here: 613 us
  Pallas kernels  613 us (100%)
    pallas_call x1, Pallas kernels, step(): pl.pallas_call(functools.partial(kernel, count), out_shape=[pltpu.VMEM(*o...  593 us
    pallas_call x1, Pallas kernels, step(): pl.pallas_call(finish, out_shape=[jax.ShapeDtypeStruct(*one) for one in r...  19.5 us

profile of v5, /device:TPU:0, one launch (start us, length us, event | category | flops | bytes accessed | tf_op | source)
XLA Modules:
  0.0 613.3 jit_solution(14710511025836623648)
XLA Ops:
  0.6 593.2 %step.1 = (bf16[2,1024,3328]{2,1,0:T(8,128)(2,1)S(1)}, bf16[2,1024,3328]{2,1,0:T(8,128)(2,1)S(1)}, bf16[2,3328,1024]{2,1,0:T(8,128)(2,1)S(1)}, f32[2,128,3328]{2...) custom-call(bf16[1,2,1024,3328]{3,2,1,0:T(8,128)(2,1)} %refs_0_.1, ...), custom_call_target="tpu_custom_call" | custom-call | tf_op jit(solution)/shard_map/step/pallas_call | solution.py:458
  593.9 19.5 %finish.1 = (bf16[2,1024,3328]{2,1,0:T(8,128)(2,1)}, bf16[2,1024,3328]{2,1,0:T(8,128)(2,1)}, bf16[2,3328,1024]{2,1,0:T(8,128)(2,1)}, f32[2,128,3328]{2,1,0:T(8,1...) custom-call(bf16[2,1024,3328]{2,1,0:T(8,128)(2,1)S(1)} %get-tuple-el, ...), custom_call_target="tpu_custom_call" | custom-call | tf_op jit(solution)/shard_map/finish/pallas_call | solution.py:469
